TPU v7x, 128 devices: a whole 4x4x4 slice. The times are simulated.
128 devices in a mesh: pod: 1, dp: 64 (over z, y, x), tp: 2 (over core).
Axes of the slice: x: 4, y: 4, z: 4, core: 2. Of those that a mesh axis runs over, the one named last changes fastest.
Arguments:
- tokens: bfloat16 [128, 256, 2048], P(('pod', 'dp'))
- seg_ids: int32 [128, 256], P(('pod', 'dp'))
- grad_out: bfloat16 [128, 256, 2048], P(('pod', 'dp'))
- gain_attn: float32 [2048], replicated
- gain_mlp: float32 [2048], replicated
- w_query: bfloat16 [2048, 2048], P(None, 'tp')
- w_key: bfloat16 [2048, 1024], P(None, 'tp')
- w_value: bfloat16 [2048, 1024], P(None, 'tp')
- w_out: bfloat16 [2048, 2048], P('tp')
- w_gate: bfloat16 [2048, 6144], P(None, 'tp')
- w_up: bfloat16 [2048, 6144], P(None, 'tp')
- w_down: bfloat16 [6144, 2048], P('tp')
Outputs:
- output 1: bfloat16 [128, 256, 2048], P(('pod', 'dp'))
- output 2: bfloat16 [128, 256, 2048], P(('pod', 'dp'))
- output 3: float32 [2048], P('pod')
- output 4: float32 [2048], P('pod')
- output 5: float32 [2048, 2048], P(('pod', 'dp'), 'tp')
- output 6: float32 [2048, 1024], P(('pod', 'dp'), 'tp')
- output 7: float32 [2048, 1024], P(('pod', 'dp'), 'tp')
- output 8: float32 [2048, 2048], P(('pod', 'tp', 'dp'))
- output 9: float32 [2048, 6144], P(('pod', 'dp'), 'tp')
- output 10: float32 [2048, 6144], P(('pod', 'dp'), 'tp')
- output 11: float32 [6144, 2048], P(('pod', 'tp', 'dp'))
All inputs are finite; a program needn't handle non-finite values.
Results may differ from a plain program's by a relative error of at most 0.02.
Values are sent between devices in bfloat16 or wider.
A program may use at most 1 GiB of HBM per device.

v0:
```python
import functools
import jax
import jax.numpy as jnp
from jax import lax
from jax.experimental import pallas as pl
from jax.experimental.pallas import tpu as pltpu
from jax.sharding import PartitionSpec as P


HEAD_DIM = 128
NORM_EPS = 1e-5
STEPS = (1, 3, 2)
STRIDE = {"z": 16, "y": 4, "x": 1}


def chip_coords():
    chip = lax.axis_index("dp")
    return {"z": chip // 16, "y": (chip // 4) % 4, "x": chip % 4}


def to_chip(chip, **coord):
    parts = {"z": chip // 16, "y": (chip // 4) % 4, "x": chip % 4}
    parts.update(coord)
    return 16 * (parts["z"] % 4) + 4 * (parts["y"] % 4) + parts["x"] % 4


def coord_of(chip, axis):
    return (chip // STRIDE[axis]) % 4


def shift(values, axis, step):
    pairs = [(c, to_chip(c, **{axis: coord_of(c, axis) + step})) for c in range(64)]
    return lax.ppermute(values, "dp", pairs)


def swap_cores(values):
    return lax.ppermute(values, "tp", [(0, 1), (1, 0)])


def sum_cores(part):
    other = swap_cores(part)
    return lax.reduce_precision(part.astype(jnp.float32) + other.astype(jnp.float32), 8, 7)


def pick(values, index, dim):
    return lax.dynamic_index_in_dim(values, index % values.shape[dim], dim, keepdims=False)


def gather_tokens(values, axis):
    return [values] + [shift(values, axis, d) for d in STEPS]


def send_row(values, axis):
    half = values.shape[0] // 2
    row = lax.dynamic_slice_in_dim(values, lax.axis_index("tp") * half, half, 0)
    return [shift(row, axis, d) for d in STEPS]


def share_rows(values, direct):
    return [values] + direct + [swap_cores(v) for v in direct]


def exchange_columns(values, axis, at):
    width = values.shape[1] // 4
    return [shift(lax.dynamic_slice_in_dim(values, ((at[axis] + d) % 4) * width, width, 1), axis, d) for d in STEPS]


def add_parts(parts):
    return parts[0] + parts[1] + parts[2] + parts[3]


def exchange_kernel(routes, *refs):
    n = len(routes)
    sources, targets, (send_sem, recv_sem) = refs[:n], refs[n:2 * n], refs[2 * n:]
    chip = lax.axis_index("dp")

    def chip_at(offset, sign):
        return to_chip(chip, **{a: coord_of(chip, a) + sign * offset[k] + 4 for k, a in enumerate("zyx")})

    barrier = pltpu.get_barrier_semaphore()
    offsets = sorted(set(routes))
    for offset in offsets:
        pl.semaphore_signal(barrier, inc=1, device_id={"dp": chip_at(offset, -1)}, device_id_type=pl.DeviceIdType.MESH)
    pl.semaphore_wait(barrier, len(offsets))
    copies = []
    for k, offset in enumerate(routes):
        copies.append(pltpu.make_async_remote_copy(
            src_ref=sources[k], dst_ref=targets[k], send_sem=send_sem.at[k], recv_sem=recv_sem.at[k],
            device_id={"dp": chip_at(offset, 1)}, device_id_type=pl.DeviceIdType.MESH))
    for copy in copies:
        copy.start()
    for copy in copies:
        copy.wait()


def along(axis):
    return [tuple(d if a == axis else 0 for a in "zyx") for d in (2, 1, 3)]


def exchange(groups, call_id):
    entries = [(g, offset, value) for g, group in enumerate(groups) for offset, value in group]
    values = [value for _, _, value in entries]
    any_spec = pl.BlockSpec(memory_space=pl.ANY)
    n = len(values)
    sent = sum(v.size * v.dtype.itemsize for v in values)
    out = pl.pallas_call(
        functools.partial(exchange_kernel, [offset for _, offset, _ in entries]),
        in_specs=[any_spec] * n,
        out_specs=[any_spec] * n,
        out_shape=[jax.ShapeDtypeStruct(v.shape, v.dtype) for v in values],
        scratch_shapes=[pltpu.SemaphoreType.DMA((n,)), pltpu.SemaphoreType.DMA((n,))],
        compiler_params=pltpu.CompilerParams(collective_id=call_id, has_side_effects=True),
        cost_estimate=pl.CostEstimate(flops=0, bytes_accessed=2 * sent, transcendentals=0),
    )(*values)
    out = lax.optimization_barrier(out)
    got = [{} for _ in groups]
    for (g, offset, _), value in zip(entries, out):
        got[g][offset] = value
    return got


def line_group(axis, turn):
    return [(offset, turn[sum(offset)]) for offset in along(axis)]


def line_values(got):
    by_distance = {sum(offset): value for offset, value in got.items()}
    return [by_distance[d] for d in (1, 2, 3)]


def in_source_order(own, received, here):
    stacked = jnp.stack([own] + received)
    return [pick(stacked, here - b, 0) for b in range(4)]


def load_plan(own_rows, shared):
    half = own_rows // 2
    if not shared:
        return [(k, "all", own_rows, own_rows * k) for k in range(4)]
    plan = [(0, "all", own_rows, 0)]
    for group, which in enumerate(("mine", "other")):
        for k in range(3):
            plan.append((k + 1, which, half, own_rows + half * (3 * group + k)))
    return plan


def row_start(which, half, core):
    if which == "all":
        return 0
    return pl.multiple_of((core if which == "mine" else 1 - core) * half, half)


def dot_tokens(left, right):
    return lax.dot_general(left, right, (((0,), (0,)), ((), ())), preferred_element_type=jnp.float32)


def column_kernel(hi_mode, width, n_chunks, info, *refs):
    lefts, rights, outs, refs = refs[:7], refs[7:11], refs[11:15], refs[15:]
    left_buf, right_buf, acc, left_sem, right_sem, out_sem = refs
    hi_at, lo_at, block, core = info[0], info[1], info[2], info[3]
    n_own = lefts[0].shape[0]
    half = n_own // 2
    plan = load_plan(n_own, True)

    right_copies = []
    for k, (source, which, rows, first) in enumerate(plan):
        whole = rights[source].shape[1] == width
        col = 0 if whole else pl.multiple_of(block * width, 128)
        right_copies.append(pltpu.make_async_copy(
            rights[source].at[pl.ds(row_start(which, half, core), rows), pl.ds(col, width)],
            right_buf.at[pl.ds(first, rows), :], right_sem.at[k]))
    for copy in right_copies:
        copy.start()

    def row_block(step):
        return lax.rem(hi_at + step + 1, 4)

    def left_copies(step, slot):
        col = pl.multiple_of(row_block(step) * 512, 512)
        for k, (source, which, rows, first) in enumerate(plan):
            yield pltpu.make_async_copy(
                lefts[k].at[:, pl.ds(col, 512)], left_buf.at[slot, pl.ds(first, rows), :], left_sem.at[slot, k])

    for copy in left_copies(0, 0):
        copy.start()
    for copy in right_copies:
        copy.wait()

    def lo_copies(step):
        rows = 128 // n_chunks
        for d in range(4):
            for k in range(n_chunks):
                first = pl.multiple_of(k * 128 + lax.rem(lo_at + d, 4) * rows, rows)
                yield pltpu.make_async_copy(
                    acc.at[step, pl.ds(first, rows), :], outs[d].at[row_block(step), pl.ds(k * rows, rows), :], out_sem.at[step, d, k])

    def hi_copy(step, d):
        return pltpu.make_async_copy(acc.at[step], outs[d], out_sem.at[step, 0, 0])

    tile = 512 if width % 512 == 0 else 256

    @pl.loop(0, 4)
    def _(step):
        slot = lax.rem(step, 2)

        @pl.when(step < 3)
        def _():
            for copy in left_copies(step + 1, 1 - slot):
                copy.start()

        for copy in left_copies(step, slot):
            copy.wait()

        for n in range(width // tile):
            cols = pl.ds(n * tile, tile)
            acc[step, :, cols] = dot_tokens(left_buf[slot], right_buf[:, cols])
        if hi_mode:
            for k in range(4):
                @pl.when(step == k)
                def _():
                    hi_copy(k, (k + 1) % 4).start()
        else:
            for copy in lo_copies(step):
                copy.start()

    for step in range(4):
        if hi_mode:
            hi_copy(step, (step + 1) % 4).wait()
        else:
            for copy in lo_copies(step):
                copy.wait()


def column_parts(lefts, rights, width, info, hi_mode, n_chunks):
    n_tok = 4 * lefts[0].shape[0]
    any_spec = pl.BlockSpec(memory_space=pl.ANY)
    f32 = jnp.float32
    return pl.pallas_call(
        functools.partial(column_kernel, hi_mode, width, n_chunks),
        grid_spec=pltpu.PrefetchScalarGridSpec(
            num_scalar_prefetch=1,
            grid=(1,),
            in_specs=[any_spec] * (len(lefts) + len(rights)),
            out_specs=[any_spec] * 4,
            scratch_shapes=[
                pltpu.VMEM((2, n_tok, 512), jnp.bfloat16),
                pltpu.VMEM((n_tok, width), jnp.bfloat16),
                pltpu.VMEM((4, 512, width), f32),
                pltpu.SemaphoreType.DMA((2, 7)),
                pltpu.SemaphoreType.DMA((7,)),
                pltpu.SemaphoreType.DMA((4, 4, 4)),
            ],
        ),
        out_shape=[jax.ShapeDtypeStruct((512, width) if hi_mode else (4, 128, width), f32)] * 4,
        compiler_params=pltpu.CompilerParams(vmem_limit_bytes=32 << 20),
        cost_estimate=pl.CostEstimate(flops=2 * n_tok * 2048 * width, bytes_accessed=20 << 20, transcendentals=0),
    )(info, *lefts, *rights)


def row_kernel(shared, hi_mode, width, info, *refs):
    lefts, refs = refs[:4], refs[4:]
    n_right = 7 if shared else 4
    rights, refs = refs[:n_right], refs[n_right:]
    outs, refs = refs[:4], refs[4:]
    left_buf, right_buf, acc, left_sem, right_sem, out_sem = refs
    p_at, block, core = info[0], info[2], info[3]
    n_own = rights[0].shape[0]
    half = n_own // 2
    rows_each = width // 16
    plan = load_plan(n_own, shared)
    left_copies = []
    for k, (source, which, rows, first) in enumerate(plan):
        col = pl.multiple_of(block * width, 128) if source == 0 else 0
        left_copies.append(pltpu.make_async_copy(
            lefts[source].at[pl.ds(row_start(which, half, core), rows), pl.ds(col, width)],
            left_buf.at[pl.ds(first, rows), :], left_sem.at[k]))
    for copy in left_copies:
        copy.start()

    def right_copies(step, slot):
        col = pl.multiple_of(step * 512, 512)
        for k, (source, which, rows, first) in enumerate(plan):
            ref = rights[k] if shared else rights[source]
            yield pltpu.make_async_copy(
                ref.at[:, pl.ds(col, 512)], right_buf.at[slot, pl.ds(first, rows), :], right_sem.at[slot, k])

    for copy in right_copies(0, 0):
        copy.start()
    for copy in left_copies:
        copy.wait()

    def out_copies(step):
        cols = pl.ds(pl.multiple_of(step * 512, 512), 512)
        for d in range(4):
            slot = lax.rem(p_at + d, 4)
            if hi_mode:
                first = pl.multiple_of(slot * (4 * rows_each), 8)
                yield pltpu.make_async_copy(
                    acc.at[step, pl.ds(first, 4 * rows_each), :], outs[d].at[:, cols], out_sem.at[step, d, 0])
            else:
                for hi in range(4):
                    first = pl.multiple_of(hi * (4 * rows_each) + slot * rows_each, 8)
                    yield pltpu.make_async_copy(
                        acc.at[step, pl.ds(first, rows_each), :], outs[d].at[hi, :, cols], out_sem.at[step, d, hi])

    @pl.loop(0, 4)
    def _(step):
        slot = lax.rem(step, 2)

        @pl.when(step < 3)
        def _():
            for copy in right_copies(step + 1, 1 - slot):
                copy.start()

        for copy in right_copies(step, slot):
            copy.wait()
        acc[step] = dot_tokens(left_buf[...], right_buf[slot])
        for copy in out_copies(step):
            copy.start()

    for step in range(4):
        for copy in out_copies(step):
            copy.wait()


def row_parts(lefts, rights, width, info, shared, hi_mode):
    n_tok = 4 * rights[0].shape[0]
    any_spec = pl.BlockSpec(memory_space=pl.ANY)
    f32 = jnp.float32
    rows_each = width // 16
    shape = (4 * rows_each, 2048) if hi_mode else (4, rows_each, 2048)
    return pl.pallas_call(
        functools.partial(row_kernel, shared, hi_mode, width),
        grid_spec=pltpu.PrefetchScalarGridSpec(
            num_scalar_prefetch=1,
            grid=(1,),
            in_specs=[any_spec] * (len(lefts) + len(rights)),
            out_specs=[any_spec] * 4,
            scratch_shapes=[
                pltpu.VMEM((n_tok, width), jnp.bfloat16),
                pltpu.VMEM((2, n_tok, 512), jnp.bfloat16),
                pltpu.VMEM((4, width, 512), f32),
                pltpu.SemaphoreType.DMA((7,)),
                pltpu.SemaphoreType.DMA((2, 7)),
                pltpu.SemaphoreType.DMA((4, 4, 4)),
            ],
        ),
        out_shape=[jax.ShapeDtypeStruct(shape, f32)] * 4,
        compiler_params=pltpu.CompilerParams(vmem_limit_bytes=40 << 20),
        cost_estimate=pl.CostEstimate(flops=2 * n_tok * 2048 * width, bytes_accessed=20 << 20, transcendentals=0),
    )(info, *lefts, *rights)


def rms_scale(values, gain):
    mean_square = jnp.mean(values * values, axis=-1, keepdims=True)
    return values * lax.rsqrt(mean_square + NORM_EPS) * gain


def gate_mix(gate_pre, up_pre):
    return (jax.nn.silu(gate_pre.astype(jnp.float32)) * up_pre.astype(jnp.float32)).astype(jnp.bfloat16)


def masked_probs(query, key_t, allowed):
    scores = lax.dot_general(query, key_t, (((1,), (1,)), ((), ())), preferred_element_type=jnp.float32) * (HEAD_DIM ** -0.5)
    scores = jnp.where(allowed, scores, -1e30)
    weights = jnp.exp(scores - jnp.max(scores, axis=-1, keepdims=True))
    return weights / jnp.sum(weights, axis=-1, keepdims=True)


def visible(seg_col, seg_row):
    n = seg_row.shape[1]
    query_pos = lax.broadcasted_iota(jnp.int32, (n, n), 0)
    key_pos = lax.broadcasted_iota(jnp.int32, (n, n), 1)
    return (key_pos <= query_pos) & (seg_col == seg_row)


def attend_kernel(seg_col_ref, seg_row_ref, query_ref, key_ref, value_ref, context_ref):
    allowed = visible(seg_col_ref[0], seg_row_ref[0])
    for g in range(query_ref.shape[1] // HEAD_DIM):
        head = pl.ds(g * HEAD_DIM, HEAD_DIM)
        probs = masked_probs(query_ref[:, head], key_ref[...], allowed).astype(jnp.bfloat16)
        context_ref[:, head] = jnp.dot(probs, value_ref[...], preferred_element_type=jnp.float32).astype(jnp.bfloat16)


def attend_back_kernel(seg_col_ref, seg_row_ref, query_ref, key_ref, value_ref, grad_ref, d_query_ref, d_key_ref, d_value_ref):
    allowed = visible(seg_col_ref[0], seg_row_ref[0])
    d_key = d_value = 0.0
    for g in range(query_ref.shape[1] // HEAD_DIM):
        head = pl.ds(g * HEAD_DIM, HEAD_DIM)
        query, grad = query_ref[:, head], grad_ref[:, head]
        probs = masked_probs(query, key_ref[...], allowed)
        d_value = d_value + dot_tokens(probs.astype(jnp.bfloat16), grad)
        d_probs = lax.dot_general(grad, value_ref[...], (((1,), (1,)), ((), ())), preferred_element_type=jnp.float32)
        d_probs = d_probs.astype(jnp.bfloat16).astype(jnp.float32)
        d_scores = probs * (d_probs - jnp.sum(d_probs * probs, axis=-1, keepdims=True))
        d_scores = (jnp.where(allowed, d_scores, 0.0) * (HEAD_DIM ** -0.5)).astype(jnp.bfloat16)
        d_query_ref[:, head] = jnp.dot(d_scores, key_ref[...], preferred_element_type=jnp.float32).astype(jnp.bfloat16)
        d_key = d_key + dot_tokens(d_scores, query)
    d_key_ref[...] = d_key.astype(jnp.bfloat16)
    d_value_ref[...] = d_value.astype(jnp.bfloat16)


def attention_call(body, seg_ids, arrays, outs, n_dots):
    n_rows, seq_len = seg_ids.shape
    kv_heads = arrays[1].shape[1] // HEAD_DIM
    block = lambda v: pl.BlockSpec((seq_len, v.shape[1] // kv_heads), lambda r, h: (r, h))
    return pl.pallas_call(
        body,
        grid=(n_rows, kv_heads),
        in_specs=[pl.BlockSpec((1, seq_len, 1), lambda r, h: (r, 0, 0)), pl.BlockSpec((1, 1, seq_len), lambda r, h: (r, 0, 0))]
        + [block(v) for v in arrays],
        out_specs=[block(v) for v in outs],
        out_shape=[jax.ShapeDtypeStruct(v.shape, jnp.bfloat16) for v in outs],
        cost_estimate=pl.CostEstimate(
            flops=2 * n_dots * n_rows * seq_len * seq_len * arrays[0].shape[1] * 4, bytes_accessed=8 << 20, transcendentals=0),
    )(seg_ids[:, :, None], seg_ids[:, None, :], *arrays)


def project(values, weight):
    return jnp.einsum("...d,df->...f", values, weight, preferred_element_type=jnp.float32)


def project_back(grads, weight):
    return jnp.einsum("...f,df->...d", grads, weight, preferred_element_type=jnp.float32)


def layer_step(tokens, seg_ids, grad_out, gain_attn, gain_mlp, w_query, w_key, w_value, w_out, w_gate, w_up, w_down):
    n_tok = tokens.shape[0] * tokens.shape[1]
    width = tokens.shape[2]
    at = chip_coords()
    flat = lambda v: v.reshape(n_tok, v.shape[-1])
    out_shape = tokens.shape
    grad_out = flat(grad_out)
    core = lax.axis_index("tp")
    info = lambda p_at, lo_at, block: jnp.stack([at[p_at], at[lo_at], at[block], core]).astype(jnp.int32)

    grad_all = gather_tokens(grad_out, "z")
    x_float = flat(tokens).astype(jnp.float32)
    norm_attn, attn_norm_vjp = jax.vjp(rms_scale, x_float, gain_attn)
    attn_in = norm_attn.astype(jnp.bfloat16)
    attn_in_sent = send_row(attn_in, "x")
    query = project(attn_in, w_query).astype(jnp.bfloat16)
    key_proj = project(attn_in, w_key).astype(jnp.bfloat16)
    value_proj = project(attn_in, w_value).astype(jnp.bfloat16)
    (context,) = attention_call(attend_kernel, seg_ids, (query, key_proj, value_proj), (query,), 2)
    attn_sum = sum_cores(project(context, w_out).astype(jnp.bfloat16))
    hidden_float = (x_float + attn_sum).astype(jnp.bfloat16).astype(jnp.float32)
    norm_mlp, mlp_norm_vjp = jax.vjp(rms_scale, hidden_float, gain_mlp)
    mlp_in = norm_mlp.astype(jnp.bfloat16)
    mlp_in_sent_x, mlp_in_sent_y = send_row(mlp_in, "x"), send_row(mlp_in, "y")
    attn_in_all = share_rows(attn_in, attn_in_sent)
    gate_pre = project(mlp_in, w_gate).astype(jnp.bfloat16)
    up_pre = project(mlp_in, w_up).astype(jnp.bfloat16)
    mixed_act, mix_vjp = jax.vjp(gate_mix, gate_pre, up_pre)
    d_mixed = project_back(grad_out, w_down).astype(jnp.bfloat16)
    d_gate, d_up = mix_vjp(d_mixed)
    d_gate_all = [d_gate] + exchange_columns(d_gate, "x", at)
    d_up_all = [d_up] + exchange_columns(d_up, "y", at)
    mixed_all = [mixed_act] + exchange_columns(mixed_act, "z", at)
    context_all = [context] + exchange_columns(context, "z", at)
    d_mlp_part = (project_back(d_gate, w_gate) + project_back(d_up, w_up)).astype(jnp.bfloat16)
    d_mlp_in = sum_cores(d_mlp_part)
    mlp_in_x, mlp_in_y = share_rows(mlp_in, mlp_in_sent_x), share_rows(mlp_in, mlp_in_sent_y)
    mlp_part = project(mixed_act, w_down).astype(jnp.bfloat16)
    mlp_sum = sum_cores(mlp_part)
    layer_out = (hidden_float + mlp_sum).astype(jnp.bfloat16).reshape(out_shape)
    d_hidden_part, gain_mlp_part = mlp_norm_vjp(d_mlp_in)
    d_hidden = grad_out.astype(jnp.float32) + d_hidden_part
    d_hidden_b = d_hidden.astype(jnp.bfloat16)
    d_hidden_sent = send_row(d_hidden_b, "z")
    d_context = project_back(d_hidden_b, w_out).astype(jnp.bfloat16)
    d_query, d_key, d_value = attention_call(
        attend_back_kernel, seg_ids, (query, key_proj, value_proj, d_context), (query, key_proj, value_proj), 5)
    n_q = w_query.shape[1] // 4
    n_k = w_key.shape[1] // 4
    n_own = width // 64

    def qkv_block(b):
        return jnp.concatenate(
            [lax.dynamic_slice_in_dim(v, (b % 4) * (v.shape[-1] // 4), v.shape[-1] // 4, 1) for v in (d_query, d_key, d_value)], axis=1)

    qkv_all = [qkv_block(at["x"])] + [shift(qkv_block(at["x"] + d), "x", d) for d in STEPS]
    d_hidden_all = share_rows(d_hidden_b, d_hidden_sent)
    d_attn_part = (project_back(d_query, w_query) + project_back(d_key, w_key) + project_back(d_value, w_value)).astype(jnp.bfloat16)
    d_attn_in = sum_cores(d_attn_part)
    d_tokens_part, gain_attn_part = attn_norm_vjp(d_attn_in)
    grad_tokens = (d_hidden + d_tokens_part).astype(jnp.bfloat16).reshape(out_shape)
    gains = jnp.stack([gain_attn_part, gain_mlp_part])

    down_parts = row_parts(mixed_all, grad_all, mixed_act.shape[-1] // 4, info("y", "y", "z"), False, True)
    down_sent = [shift(down_parts[d], "y", d) for d in STEPS]
    gate_parts = column_parts(mlp_in_x, d_gate_all, d_gate.shape[-1] // 4, info("z", "y", "x"), True, 1)
    gate_sent = [shift(gate_parts[d], "z", d) for d in STEPS]
    up_parts = column_parts(mlp_in_y, d_up_all, d_up.shape[-1] // 4, info("z", "x", "y"), False, 4)
    up_sent = [shift(up_parts[d], "x", d) for d in STEPS]
    out_parts = row_parts(context_all, d_hidden_all, context.shape[-1] // 4, info("x", "x", "z"), True, False)
    out_sent = [shift(out_parts[d], "x", d) for d in STEPS]
    qkv_parts = column_parts(attn_in_all, qkv_all, qkv_all[1].shape[1], info("z", "y", "x"), False, 1)
    qkv_sent = [shift(qkv_parts[d], "y", d) for d in STEPS]
    g_down = add_parts([down_parts[0]] + down_sent).reshape(4, -1, width)
    g_gate = add_parts([gate_parts[0]] + gate_sent).reshape(4, 128, -1)
    g_up = add_parts([up_parts[0]] + up_sent)
    g_out = add_parts([out_parts[0]] + out_sent)
    g_qkv = add_parts([qkv_parts[0]] + qkv_sent)

    def turns(values, here, dim=0):
        return [pick(values, here + d, dim) for d in range(4)]

    gate_turn, up_turn, down_turn = turns(g_gate, at["y"]), turns(g_up, at["z"]), turns(g_down, at["x"])
    qkv_turn, out_turn = turns(g_qkv, at["z"]), turns(g_out, at["y"])
    got = exchange([
        line_group("y", gate_turn), line_group("z", up_turn), line_group("x", down_turn), line_group("z", qkv_turn),
        line_group("y", out_turn), line_group("x", [gains] * 4),
    ], 1)
    got = [line_values(g) for g in got]
    grad_down = add_parts([down_turn[0]] + got[2])
    grad_out_w = add_parts([out_turn[0]] + got[4])
    gains = add_parts(in_source_order(gains, got[5], at["x"]))
    gate_turn = turns(add_parts([gate_turn[0]] + got[0]).reshape(4, n_own, -1), at["x"])
    up_turn = turns(add_parts([up_turn[0]] + got[1]).reshape(4, n_own, -1), at["y"])
    qkv_turn = turns(add_parts([qkv_turn[0]] + got[3]).reshape(4, n_own, -1), at["x"])
    plane = [(dz, dy, 0) for dz in range(4) for dy in range(4) if dz or dy]
    got = exchange([
        line_group("x", gate_turn), line_group("y", up_turn), line_group("x", qkv_turn), [(offset, gains) for offset in plane],
    ], 2)
    grad_gate = jnp.concatenate(in_source_order(gate_turn[0], line_values(got[0]), at["x"]), axis=1)
    grad_up = jnp.concatenate(in_source_order(up_turn[0], line_values(got[1]), at["y"]), axis=1)
    ordered = in_source_order(qkv_turn[0], line_values(got[2]), at["x"])
    in_plane = jnp.stack([got[3].get((dz, dy, 0), gains) for dz in range(4) for dy in range(4)]).reshape(4, 4, 2, width)
    in_plane = jnp.stack([pick(in_plane, at["z"] - z, 0) for z in range(4)])
    in_plane = jnp.stack([pick(in_plane, at["y"] - y, 1) for y in range(4)])
    gains = jnp.sum(in_plane, axis=(0, 1))
    grad_query = jnp.concatenate([o[:, :n_q] for o in ordered], axis=1)
    grad_key = jnp.concatenate([o[:, n_q:n_q + n_k] for o in ordered], axis=1)
    grad_value = jnp.concatenate([o[:, n_q + n_k:] for o in ordered], axis=1)
    return (
        layer_out,
        grad_tokens,
        gains[0],
        gains[1],
        grad_query,
        grad_key,
        grad_value,
        grad_out_w,
        grad_gate,
        grad_up,
        grad_down,
    )


def solution(mesh):
    row_spec = P(("pod", "dp"), None, None)
    seg_spec = P(("pod", "dp"), None)
    col_spec = P(None, "tp")
    row_split = P("tp", None)
    grad_col = P(("pod", "dp"), "tp")
    grad_row = P(("pod", "tp", "dp"), None)
    gain_spec = P("pod")
    return jax.shard_map(
        layer_step,
        mesh=mesh,
        in_specs=(row_spec, seg_spec, row_spec, P(), P(), col_spec, col_spec, col_spec, row_split, col_spec, col_spec, row_split),
        out_specs=(row_spec, row_spec, gain_spec, gain_spec, grad_col, grad_col, grad_col, grad_row, grad_col, grad_col, grad_row),
        check_vma=False,
    )
```

profile of v0, /device:TPU:0, one launch (start us, length us, event | category | flops | bytes accessed | tf_op | source)
XLA Modules:
  0.0 634.0 jit_solution(9265113515835559825)
XLA Ops:
  19.5 9.5 %shard_map.203.refs_0_ = bf16[512,1024]{1,0:T(8,128)(2,1)} custom-call(s32[2,256,1]{2,1,0:T(8,128)} %copy.23.seg_col_ref, s32[2,1,256]{2,1,0:T(1,128)} %broadcast_in_dim.9.seg_row_ref, bf16[512,1024]{1,0:T(8,128)(2,1)} %convolution_convert_fusion.6.query_ref, bf16[512,512]{1,0:T(8,128)(2,1)} %convolution_convert_fusion.8.key_ref, ...), custom_call_target="tpu_custom_call" | custom-call | flops 2147483648 | bytes 8388608 | tf_op jit(solution)/shard_map/pallas_call | solution.py:407
  28.9 6.2 convolution_convert_fusion.4
  41.3 13.2 %convolution_convert_fusion = bf16[512,3072]{1,0:T(8,128)(2,1)} fusion(bf16[512,2048]{1,0:T(8,128)(2,1)} %bitcast.223, bf16[3072,2048]{1,0:T(8,128)(2,1)} %param.23), kind=kOutput, calls=%fused_computation.24 | convolution fusion | flops 6444023808 | bytes 17825792 | tf_op jit(solution)/shard_map/...f,df->...d/dot_general | solution.py:424
  61.4 10.6 %convolution_convert_fusion.1 = bf16[512,3072]{1,0:T(8,128)(2,1)S(1)} fusion(bf16[512,2048]{1,0:T(8,128)(2,1)S(1)} %fusion.10.refs_0_, bf16[2048,3072]{1,0:T(8,128)(2,1)} %param.22), kind=kOutput, calls=%fused_computation.25 | convolution fusion | flops 6444023808 | bytes 17825792 | tf_op jit(solution)/shard_map/...d,df->...f/dot_general | solution.py:420
  72.0 16.7 %fusion.1 = (bf16[512,3072]{1,0:T(8,128)(2,1)}, bf16[512,3072]{1,0:T(8,128)(2,1)S(1)}, bf16[512,3072]{1,0:T(8,128)(2,1)}) fusion(bf16[512,3072]{1,0:T(8,128)(2,1)S(1)} %copy-done.87, bf16[512,3072]{1,0:T(8,128)(2,1)S(1)} %convolution_convert_fusion.1, bf16[512,2048]{1,0:T(8,128)(2,1)S(1)} %fusion.10.refs_0_, bf16[2048,3072]{1,0:T(8,128)(2,1)} %param.21), kind=kOutput, calls=%fused_computation.13 | convolution fusion | flops 6473908224 | bytes 30408704 | tf_op jit(solution)/shard_map/...d,df->...f/dot_general | solution.py:420
  92.3 11.3 %fusion.48 = f32[512,2048]{1,0:T(8,128)} fusion(bf16[512,3072]{1,0:T(8,128)(2,1)S(1)} %get-tuple-element.154.refs_7_, bf16[2048,3072]{1,0:T(8,128)(2,1)} %param.21), kind=kOutput, calls=%fused_computation.206 | convolution fusion | flops 6442450944 | bytes 19922944 | tf_op jit(solution)/shard_map/...f,df->...d/dot_general | solution.py:424
  105.9 29.6 %collective-permute-done.38.refs_2_ = bf16[256,2048]{1,0:T(8,128)(2,1)} collective-permute-done((bf16[256,2048]{1,0:T(8,128)(2,1)}, bf16[256,2048]{1,0:T(8,128)(2,1)}, u32[]{:S(2)}, u32[]{:S(2)}) %collective-permute-start.38) | collective-permute-done | bytes 1048608 | tf_op jit(solution)/shard_map/ppermute | solution.py:33
  139.8 13.6 %add_convert_fusion.1 = bf16[512,2048]{1,0:T(8,128)(2,1)} fusion(f32[512,2048]{1,0:T(8,128)} %fusion.48, bf16[512,3072]{1,0:T(8,128)(2,1)} %get-tuple-element.153.refs_7_, bf16[2048,3072]{1,0:T(8,128)(2,1)} %param.22), kind=kOutput, calls=%fused_computation.50 | convolution fusion | flops 6444548096 | bytes 22020096 | tf_op jit(solution)/shard_map/...f,df->...d/dot_general | solution.py:424
  160.5 11.7 %convolution_convert_fusion.3 = bf16[512,2048]{1,0:T(8,128)(2,1)} fusion(bf16[512,3072]{1,0:T(8,128)(2,1)} %get-tuple-element.155.refs_0_, bf16[3072,2048]{1,0:T(8,128)(2,1)} %param.23), kind=kOutput, calls=%fused_computation.51 | convolution fusion | flops 6443499520 | bytes 17825792 | tf_op jit(solution)/shard_map/...d,df->...f/dot_general | solution.py:420
  178.7 16.1 %collective-permute-done.28.refs_1_ = bf16[512,768]{1,0:T(8,128)(2,1)S(1)} collective-permute-done((bf16[512,768]{1,0:T(8,128)(2,1)S(1)}, bf16[512,768]{1,0:T(8,128)(2,1)S(1)}, u32[]{:S(2)}, u32[]{:S(2)}) %collective-permute-start.28) | collective-permute-done | bytes 786464 | tf_op jit(solution)/shard_map/ppermute | solution.py:33
  201.2 11.1 %shard_map.207 = (f32[192,2048]{1,0:T(8,128)S(1)}, f32[192,2048]{1,0:T(8,128)S(1)}, f32[192,2048]{1,0:T(8,128)S(1)}, f32[192,2048]{1,0:T(8,128)S(1)}) custom-call(s32[4]{0:T(128)S(1)} %add_add_fusion.10.info, bf16[512,3072]{1,0:T(8,128)(2,1)} %get-tuple-element.155.refs_0_, bf16[512,768]{1,0:T(8,128)(2,1)S(1)} %collective-permute-done.28.refs_1_, ...), custom_call_target="tpu_custom_call" | custom-call | flops 6442450944 | bytes 20971520 | tf_op jit(solution)/shard_map/pallas_call | solution.py:332
  215.1 16.0 %collective-permute-done.23.refs_9_ = bf16[512,768]{1,0:T(8,128)(2,1)S(1)} collective-permute-done((bf16[512,768]{1,0:T(8,128)(2,1)}, bf16[512,768]{1,0:T(8,128)(2,1)S(1)}, u32[]{:S(2)}, u32[]{:S(2)}) %collective-permute-start.23) | collective-permute-done | bytes 786464 | tf_op jit(solution)/shard_map/ppermute | solution.py:33
  247.6 11.3 %collective-permute-done.5.refs_2_ = bf16[256,2048]{1,0:T(8,128)(2,1)} collective-permute-done((bf16[256,2048]{1,0:T(8,128)(2,1)}, bf16[256,2048]{1,0:T(8,128)(2,1)}, u32[]{:S(2)}, u32[]{:S(2)}) %collective-permute-start.5) | collective-permute-done | bytes 1048608 | tf_op jit(solution)/shard_map/ppermute | solution.py:33
  266.0 13.7 %collective-permute-done.18.refs_3_ = bf16[256,2048]{1,0:T(8,128)(2,1)S(1)} collective-permute-done((bf16[256,2048]{1,0:T(8,128)(2,1)}, bf16[256,2048]{1,0:T(8,128)(2,1)S(1)}, u32[]{:S(2)}, u32[]{:S(2)}) %collective-permute-start.18) | collective-permute-done | bytes 1048608 | tf_op jit(solution)/shard_map/ppermute | solution.py:33
  281.1 11.7 %shard_map.204 = (bf16[512,1024]{1,0:T(8,128)(2,1)}, bf16[512,512]{1,0:T(8,128)(2,1)}, bf16[512,512]{1,0:T(8,128)(2,1)}) custom-call(s32[2,256,1]{2,1,0:T(8,128)} %copy.23.seg_col_ref, s32[2,1,256]{2,1,0:T(1,128)} %broadcast_in_dim.9.seg_row_ref, bf16[512,1024]{1,0:T(8,128)(2,1)} %convolution_convert_fusion.6.query_ref, ...), custom_call_target="tpu_custom_call" | custom-call | flops 5368709120 | bytes 8388608 | tf_op jit(solution)/shard_map/pallas_call | solution.py:407
  305.0 11.3 %shard_map.205 = (f32[512,768]{1,0:T(8,128)S(1)}, f32[512,768]{1,0:T(8,128)S(1)}, f32[512,768]{1,0:T(8,128)S(1)}, f32[512,768]{1,0:T(8,128)}) custom-call(s32[4]{0:T(128)S(1)} %add_add_fusion.8.info, bf16[512,2048]{1,0:T(8,128)(2,1)S(1)} %copy-done.8, bf16[256,2048]{1,0:T(8,128)(2,1)} %collective-permute-done.4.refs_1_, ...), custom_call_target="tpu_custom_call" | custom-call | flops 6442450944 | bytes 20971520 | tf_op jit(solution)/shard_map/pallas_call | solution.py:238
  323.2 16.6 %shard_map.206 = (f32[4,128,768]{2,1,0:T(8,128)S(1)}, f32[4,128,768]{2,1,0:T(8,128)S(1)}, f32[4,128,768]{2,1,0:T(8,128)}, f32[4,128,768]{2,1,0:T(8,128)}) custom-call(s32[4]{0:T(128)S(1)} %add_add_fusion.9.info, bf16[512,2048]{1,0:T(8,128)(2,1)S(1)} %copy-done.8, bf16[256,2048]{1,0:T(8,128)(2,1)} %collective-permute-done.16.refs_1_, ...), custom_call_target="tpu_custom_call" | custom-call | flops 6442450944 | bytes 20971520 | tf_op jit(solution)/shard_map/pallas_call | solution.py:238
  340.0 29.1 %collective-permute-done.35 = f32[192,2048]{1,0:T(8,128)} collective-permute-done((f32[192,2048]{1,0:T(8,128)}, f32[192,2048]{1,0:T(8,128)}, u32[]{:S(2)}, u32[]{:S(2)}) %collective-permute-start.35) | collective-permute-done | bytes 1572896 | tf_op jit(solution)/shard_map/ppermute | solution.py:33
  372.7 4.6 fusion.49
  377.3 33.0 %collective-permute-done.44.refs_9_ = bf16[512,512]{1,0:T(8,128)(2,1)S(1)} collective-permute-done((bf16[512,512]{1,0:T(8,128)(2,1)S(1)}, bf16[512,512]{1,0:T(8,128)(2,1)S(1)}, u32[]{:S(2)}, u32[]{:S(2)}) %collective-permute-start.44) | collective-permute-done | bytes 524320 | tf_op jit(solution)/shard_map/ppermute | solution.py:33
  418.1 8.6 %shard_map.208 = (f32[4,128,512]{2,1,0:T(8,128)S(1)}, f32[4,128,512]{2,1,0:T(8,128)S(1)}, f32[4,128,512]{2,1,0:T(8,128)S(1)}, f32[4,128,512]{2,1,0:T(8,128)S(1)}) custom-call(s32[4]{0:T(128)S(1)} %add_add_fusion.8.info, bf16[512,2048]{1,0:T(8,128)(2,1)S(1)} %copy-done.6, bf16[256,2048]{1,0:T(8,128)(2,1)} %collective-permute-done.37.refs_1_, ...), custom_call_target="tpu_custom_call" | custom-call | flops 4294967296 | bytes 20971520 | tf_op jit(solution)/shard_map/pallas_call | solution.py:238
  430.9 5.8 collective-permute-done.27
  436.6 24.8 %collective-permute-done.26 = f32[4,128,768]{2,1,0:T(8,128)} collective-permute-done((f32[4,128,768]{2,1,0:T(8,128)}, f32[4,128,768]{2,1,0:T(8,128)}, u32[]{:S(2)}, u32[]{:S(2)}) %collective-permute-start.26) | collective-permute-done | bytes 1572896 | tf_op jit(solution)/shard_map/ppermute | solution.py:33
  473.0 8.8 %collective-permute-done.46 = f32[4,128,512]{2,1,0:T(8,128)S(1)} collective-permute-done((f32[4,128,512]{2,1,0:T(8,128)S(1)}, f32[4,128,512]{2,1,0:T(8,128)S(1)}, u32[]{:S(2)}, u32[]{:S(2)}) %collective-permute-start.46) | collective-permute-done | bytes 1048608 | tf_op jit(solution)/shard_map/ppermute | solution.py:33
  485.5 7.3 %collective-permute-done.52.refs_5_ = bf16[256,2048]{1,0:T(8,128)(2,1)S(1)} collective-permute-done((bf16[256,2048]{1,0:T(8,128)(2,1)S(1)}, bf16[256,2048]{1,0:T(8,128)(2,1)S(1)}, u32[]{:S(2)}, u32[]{:S(2)}) %collective-permute-start.52) | collective-permute-done | bytes 1048608 | tf_op jit(solution)/shard_map/ppermute | solution.py:33
  492.9 15.6 %collective-permute-done.53.refs_6_ = bf16[256,2048]{1,0:T(8,128)(2,1)S(1)} collective-permute-done((bf16[256,2048]{1,0:T(8,128)(2,1)S(1)}, bf16[256,2048]{1,0:T(8,128)(2,1)S(1)}, u32[]{:S(2)}, u32[]{:S(2)}) %collective-permute-start.53) | collective-permute-done | bytes 1048608 | tf_op jit(solution)/shard_map/ppermute | solution.py:33
  515.7 8.3 %collective-permute-done.51.refs_3_ = bf16[512,256]{1,0:T(8,128)(2,1)S(1)} collective-permute-done((bf16[512,256]{1,0:T(8,128)(2,1)S(1)}, bf16[512,256]{1,0:T(8,128)(2,1)S(1)}, u32[]{:S(2)}, u32[]{:S(2)}) %collective-permute-start.51) | collective-permute-done | bytes 262176 | tf_op jit(solution)/shard_map/ppermute | solution.py:33
  524.0 7.8 %shard_map.209 = (f32[4,16,2048]{2,1,0:T(8,128)S(1)}, f32[4,16,2048]{2,1,0:T(8,128)S(1)}, f32[4,16,2048]{2,1,0:T(8,128)S(1)}, f32[4,16,2048]{2,1,0:T(8,128)S(1)}) custom-call(s32[4]{0:T(128)S(1)} %add_add_fusion.11.info, bf16[512,1024]{1,0:T(8,128)(2,1)S(1)} %copy-done.10, bf16[512,256]{1,0:T(8,128)(2,1)S(1)} %collective-permute-done.49.refs_1_, ...), custom_call_target="tpu_custom_call" | custom-call | flops 2147483648 | bytes 20971520 | tf_op jit(solution)/shard_map/pallas_call | solution.py:332
  536.6 9.6 %fusion.14 = (bf16[512,2048]{1,0:T(8,128)(2,1)}, bf16[512,2048]{1,0:T(8,128)(2,1)}) fusion(bf16[2,256,2048]{2,1,0:T(8,128)(2,1)S(1)} %copy-done.37, bf16[512,2048]{1,0:T(8,128)(2,1)} %copy-done.43, bf16[512,2048]{1,0:T(8,128)(2,1)} %copy-done.41, f32[512]{0:T(512)S(1)} %multiply_multiply_fusion, f32[2048]{0:T(1024)S(1)} %copy-done.77, f32[512]{0:T(512)S(1)} %copy-done.79, ...), kind=kLoop, calls=%fused_computation.31 | loop fusion | flops 31457280 | bytes 23093248 | tf_op jit(solution)/shard_map/convert_element_type | solution.py:487
  548.3 10.9 %collective-permute-done.59 = f32[4,16,2048]{2,1,0:T(8,128)S(1)} collective-permute-done((f32[4,16,2048]{2,1,0:T(8,128)S(1)}, f32[4,16,2048]{2,1,0:T(8,128)S(1)}, u32[]{:S(2)}, u32[]{:S(2)}) %collective-permute-start.59) | collective-permute-done | bytes 524320 | tf_op jit(solution)/shard_map/ppermute | solution.py:33
  560.0 33.2 %shard_map.210 = (f32[128,768]{1,0:T(8,128)}, f32[128,768]{1,0:T(8,128)}, f32[128,768]{1,0:T(8,128)}, f32[128,768]{1,0:T(8,128)}, f32[128,768]{1,0:T(8,128)}, /*...) custom-call(f32[128,768]{1,0:T(8,128)} %get-tuple-element.175.refs_0, ...), custom_call_target="tpu_custom_call" | custom-call | bytes 9535488 | tf_op jit(solution)/shard_map/pallas_call | solution.py:106
  600.1 14.2 %shard_map.211 = (f32[32,768]{1,0:T(8,128)}, f32[32,768]{1,0:T(8,128)}, f32[32,768]{1,0:T(8,128)}, f32[32,768]{1,0:T(8,128)}, f32[32,768]{1,0:T(8,128)}, /*index...) custom-call(f32[32,768]{1,0:T(8,128)} %get-tuple-element.212.refs_0_, ...), custom_call_target="tpu_custom_call" | custom-call | bytes 2064384 | tf_op jit(solution)/shard_map/pallas_call | solution.py:106
  (382 shorter events, 179.3 us)
Async XLA Ops:
  0.7 135.4 %collective-permute-start.31 = (bf16[512,2048]{1,0:T(8,128)(2,1)}, bf16[512,2048]{1,0:T(8,128)(2,1)}, u32[]{:S(2)}, u32[]{:S(2)}) collective-permute-start(bf16[512,2048]{1,0:T(8,128)(2,1)} %bitcast.221), channel_id=1, source_target_pairs={{0,32},{2,34},{4,36},{6,38},{8,40},{10,42},{12,44},{14,46},{16,48}... | collective-permute-start | bytes 6291464 | tf_op jit(solution)/shard_map/ppermute | solution.py:33
  2.8 135.6 %collective-permute-start.32 = (bf16[512,2048]{1,0:T(8,128)(2,1)}, bf16[512,2048]{1,0:T(8,128)(2,1)}, u32[]{:S(2)}, u32[]{:S(2)}) collective-permute-start(bf16[512,2048]{1,0:T(8,128)(2,1)} %bitcast.222), channel_id=1, source_target_pairs={{0,96},{2,98},{4,100},{6,102},{8,104},{10,106},{12,108},{14,110},{... | collective-permute-start | bytes 6291464 | tf_op jit(solution)/shard_map/ppermute | solution.py:33
  37.5 66.1 %collective-permute-start.37 = (bf16[256,2048]{1,0:T(8,128)(2,1)}, bf16[256,2048]{1,0:T(8,128)(2,1)}, u32[]{:S(2)}, u32[]{:S(2)}) collective-permute-start(bf16[256,2048]{1,0:T(8,128)(2,1)} %constant_dynamic-slice_fusion.27), channel_id=1, source_target_pairs={{0,2},{2,4},{4,6},{6,0},{8,10},{10,12},{12,14},{14,8},{16,18},{18,... | collective-permute-start | bytes 3145736 | tf_op jit(solution)/shard_map/ppermute | solution.py:33
  39.9 48.8 %collective-permute-start.49 = (bf16[512,256]{1,0:T(8,128)(2,1)}, bf16[512,256]{1,0:T(8,128)(2,1)S(1)}, u32[]{:S(2)}, u32[]{:S(2)}) collective-permute-start(bf16[512,256]{1,0:T(8,128)(2,1)} %get-tuple-element.178), channel_id=1, source_target_pairs={{0,32},{2,34},{4,36},{6,38},{8,40},{10,42},{12,44},{14,46},{16,48}... | collective-permute-start | bytes 786440 | tf_op jit(solution)/shard_map/ppermute | solution.py:33
  88.7 46.8 %collective-permute-start.38 = (bf16[256,2048]{1,0:T(8,128)(2,1)}, bf16[256,2048]{1,0:T(8,128)(2,1)}, u32[]{:S(2)}, u32[]{:S(2)}) collective-permute-start(bf16[256,2048]{1,0:T(8,128)(2,1)} %constant_dynamic-slice_fusion.27), channel_id=1, source_target_pairs={{0,6},{2,0},{4,2},{6,4},{8,14},{10,8},{12,10},{14,12},{16,22},{18,... | collective-permute-start | bytes 3145736 | tf_op jit(solution)/shard_map/ppermute | solution.py:33
  90.5 45.1 %collective-permute-start.39 = (bf16[256,2048]{1,0:T(8,128)(2,1)}, bf16[256,2048]{1,0:T(8,128)(2,1)}, u32[]{:S(2)}, u32[]{:S(2)}) collective-permute-start(bf16[256,2048]{1,0:T(8,128)(2,1)} %constant_dynamic-slice_fusion.27), channel_id=1, source_target_pairs={{0,4},{2,6},{4,0},{6,2},{8,12},{10,14},{12,8},{14,10},{16,20},{18,... | collective-permute-start | bytes 3145736 | tf_op jit(solution)/shard_map/ppermute | solution.py:33
  103.6 51.7 %collective-permute-start.33 = (bf16[512,2048]{1,0:T(8,128)(2,1)S(1)}, bf16[512,2048]{1,0:T(8,128)(2,1)}, u32[]{:S(2)}, u32[]{:S(2)}) collective-permute-start(bf16[512,2048]{1,0:T(8,128)(2,1)S(1)} %bitcast.224), channel_id=1, source_target_pairs={{0,64},{2,66},{4,68},{6,70},{8,72},{10,74},{12,76},{14,78},{16,80}... | collective-permute-start | bytes 6291464 | tf_op jit(solution)/shard_map/ppermute | solution.py:33
  155.7 79.5 %collective-permute-start.2 = (bf16[512,2048]{1,0:T(8,128)(2,1)S(1)}, bf16[512,2048]{1,0:T(8,128)(2,1)}, u32[]{:S(2)}, u32[]{:S(2)}) collective-permute-start(bf16[512,2048]{1,0:T(8,128)(2,1)S(1)} %copy-done.42), channel_id=1, source_target_pairs={{0,1},{1,0},{2,3},{3,2},{4,5},{5,4},{6,7},{7,6},{8,9},{9,8},{10,11... | collective-permute-start | bytes 6291464 | tf_op jit(solution)/shard_map/ppermute | solution.py:37
  157.2 37.6 %collective-permute-start.28 = (bf16[512,768]{1,0:T(8,128)(2,1)S(1)}, bf16[512,768]{1,0:T(8,128)(2,1)S(1)}, u32[]{:S(2)}, u32[]{:S(2)}) collective-permute-start(bf16[512,768]{1,0:T(8,128)(2,1)S(1)} %get-tuple-element.158), channel_id=1, source_target_pairs={{0,32},{2,34},{4,36},{6,38},{8,40},{10,42},{12,44},{14,46},{16,48}... | collective-permute-start | bytes 2359304 | tf_op jit(solution)/shard_map/ppermute | solution.py:33
  157.8 40.0 %collective-permute-start.29 = (bf16[512,768]{1,0:T(8,128)(2,1)S(1)}, bf16[512,768]{1,0:T(8,128)(2,1)S(1)}, u32[]{:S(2)}, u32[]{:S(2)}) collective-permute-start(bf16[512,768]{1,0:T(8,128)(2,1)S(1)} %get-tuple-element.157), channel_id=1, source_target_pairs={{0,96},{2,98},{4,100},{6,102},{8,104},{10,106},{12,108},{14,110},{... | collective-permute-start | bytes 2359304 | tf_op jit(solution)/shard_map/ppermute | solution.py:33
  160.5 39.1 %collective-permute-start.30 = (bf16[512,768]{1,0:T(8,128)(2,1)S(1)}, bf16[512,768]{1,0:T(8,128)(2,1)S(1)}, u32[]{:S(2)}, u32[]{:S(2)}) collective-permute-start(bf16[512,768]{1,0:T(8,128)(2,1)S(1)} %get-tuple-element.156), channel_id=1, source_target_pairs={{0,64},{2,66},{4,68},{6,70},{8,72},{10,74},{12,76},{14,78},{16,80}... | collective-permute-start | bytes 2359304 | tf_op jit(solution)/shard_map/ppermute | solution.py:33
  199.5 42.6 %collective-permute-start.4 = (bf16[256,2048]{1,0:T(8,128)(2,1)}, bf16[256,2048]{1,0:T(8,128)(2,1)}, u32[]{:S(2)}, u32[]{:S(2)}) collective-permute-start(bf16[256,2048]{1,0:T(8,128)(2,1)} %constant_dynamic-slice_fusion.37), channel_id=1, source_target_pairs={{0,2},{2,4},{4,6},{6,0},{8,10},{10,12},{12,14},{14,8},{16,18},{18,... | collective-permute-start | bytes 3145736 | tf_op jit(solution)/shard_map/ppermute | solution.py:33
  213.3 45.6 %collective-permute-start.5 = (bf16[256,2048]{1,0:T(8,128)(2,1)}, bf16[256,2048]{1,0:T(8,128)(2,1)}, u32[]{:S(2)}, u32[]{:S(2)}) collective-permute-start(bf16[256,2048]{1,0:T(8,128)(2,1)} %constant_dynamic-slice_fusion.37), channel_id=1, source_target_pairs={{0,6},{2,0},{4,2},{6,4},{8,14},{10,8},{12,10},{14,12},{16,22},{18,... | collective-permute-start | bytes 3145736 | tf_op jit(solution)/shard_map/ppermute | solution.py:33
  258.9 38.1 %collective-permute-start.8 = (bf16[256,2048]{1,0:T(8,128)(2,1)}, bf16[256,2048]{1,0:T(8,128)(2,1)}, u32[]{:S(2)}, u32[]{:S(2)}) collective-permute-start(bf16[256,2048]{1,0:T(8,128)(2,1)} %collective-permute-done.5.refs_2_), channel_id=1, source_target_pairs={{0,1},{1,0},{2,3},{3,2},{4,5},{5,4},{6,7},{7,6},{8,9},{9,8},{10,11... | collective-permute-start | bytes 3145736 | tf_op jit(solution)/shard_map/ppermute | solution.py:37
  262.1 38.7 %collective-permute-start.19 = (bf16[256,2048]{1,0:T(8,128)(2,1)}, bf16[256,2048]{1,0:T(8,128)(2,1)}, u32[]{:S(2)}, u32[]{:S(2)}) collective-permute-start(bf16[256,2048]{1,0:T(8,128)(2,1)} %collective-permute-done.16.refs_1_), channel_id=1, source_target_pairs={{0,1},{1,0},{2,3},{3,2},{4,5},{5,4},{6,7},{7,6},{8,9},{9,8},{10,11... | collective-permute-start | bytes 3145736 | tf_op jit(solution)/shard_map/ppermute | solution.py:37
  297.0 42.9 %collective-permute-start.36 = (f32[192,2048]{1,0:T(8,128)}, f32[192,2048]{1,0:T(8,128)}, u32[]{:S(2)}, u32[]{:S(2)}) collective-permute-start(f32[192,2048]{1,0:T(8,128)} %copy-done.22), channel_id=1, source_target_pairs={{0,16},{2,18},{4,20},{6,22},{8,24},{10,26},{12,28},{14,30},{16,0},... | collective-permute-start | bytes 4718600 | tf_op jit(solution)/shard_map/ppermute | solution.py:33
  299.1 70.0 %collective-permute-start.35 = (f32[192,2048]{1,0:T(8,128)}, f32[192,2048]{1,0:T(8,128)}, u32[]{:S(2)}, u32[]{:S(2)}) collective-permute-start(f32[192,2048]{1,0:T(8,128)} %copy-done.21), channel_id=1, source_target_pairs={{0,24},{2,26},{4,28},{6,30},{8,0},{10,2},{12,4},{14,6},{16,8},{18,... | collective-permute-start | bytes 4718600 | tf_op jit(solution)/shard_map/ppermute | solution.py:33
  300.8 68.2 %collective-permute-start.34 = (f32[192,2048]{1,0:T(8,128)S(1)}, f32[192,2048]{1,0:T(8,128)}, u32[]{:S(2)}, u32[]{:S(2)}) collective-permute-start(f32[192,2048]{1,0:T(8,128)S(1)} %copy-done.20), channel_id=1, source_target_pairs={{0,8},{2,10},{4,12},{6,14},{8,16},{10,18},{12,20},{14,22},{16,24},... | collective-permute-start | bytes 4718600 | tf_op jit(solution)/shard_map/ppermute | solution.py:33
  317.3 53.8 %collective-permute-start.43 = (bf16[512,512]{1,0:T(8,128)(2,1)}, bf16[512,512]{1,0:T(8,128)(2,1)S(1)}, u32[]{:S(2)}, u32[]{:S(2)}) collective-permute-start(bf16[512,512]{1,0:T(8,128)(2,1)} %pad_maximum_fusion.1), channel_id=1, source_target_pairs={{0,2},{2,4},{4,6},{6,0},{8,10},{10,12},{12,14},{14,8},{16,18},{18,... | collective-permute-start | bytes 1572872 | tf_op jit(solution)/shard_map/ppermute | solution.py:33
  339.8 77.0 %collective-permute-start.15 = (f32[512,768]{1,0:T(8,128)S(1)}, f32[512,768]{1,0:T(8,128)S(1)}, u32[]{:S(2)}, u32[]{:S(2)}) collective-permute-start(f32[512,768]{1,0:T(8,128)S(1)} %get-tuple-element.82), channel_id=1, source_target_pairs={{0,64},{2,66},{4,68},{6,70},{8,72},{10,74},{12,76},{14,78},{16,80}... | collective-permute-start | bytes 4718600 | tf_op jit(solution)/shard_map/ppermute | solution.py:33
  339.9 86.8 %collective-permute-start.14 = (f32[512,768]{1,0:T(8,128)}, f32[512,768]{1,0:T(8,128)S(1)}, u32[]{:S(2)}, u32[]{:S(2)}) collective-permute-start(f32[512,768]{1,0:T(8,128)} %get-tuple-element.81), channel_id=1, source_target_pairs={{0,96},{2,98},{4,100},{6,102},{8,104},{10,106},{12,108},{14,110},{... | collective-permute-start | bytes 4718600 | tf_op jit(solution)/shard_map/ppermute | solution.py:33
  369.1 59.8 %collective-permute-start.13 = (f32[512,768]{1,0:T(8,128)S(1)}, f32[512,768]{1,0:T(8,128)}, u32[]{:S(2)}, u32[]{:S(2)}) collective-permute-start(f32[512,768]{1,0:T(8,128)S(1)} %get-tuple-element.80), channel_id=1, source_target_pairs={{0,32},{2,34},{4,36},{6,38},{8,40},{10,42},{12,44},{14,46},{16,48}... | collective-permute-start | bytes 4718600 | tf_op jit(solution)/shard_map/ppermute | solution.py:33
  369.1 41.2 %collective-permute-start.44 = (bf16[512,512]{1,0:T(8,128)(2,1)S(1)}, bf16[512,512]{1,0:T(8,128)(2,1)S(1)}, u32[]{:S(2)}, u32[]{:S(2)}) collective-permute-start(bf16[512,512]{1,0:T(8,128)(2,1)S(1)} %copy-done.57), channel_id=1, source_target_pairs={{0,6},{2,0},{4,2},{6,4},{8,14},{10,8},{12,10},{14,12},{16,22},{18,... | collective-permute-start | bytes 1572872 | tf_op jit(solution)/shard_map/ppermute | solution.py:33
  371.1 39.2 %collective-permute-start.45 = (bf16[512,512]{1,0:T(8,128)(2,1)S(1)}, bf16[512,512]{1,0:T(8,128)(2,1)S(1)}, u32[]{:S(2)}, u32[]{:S(2)}) collective-permute-start(bf16[512,512]{1,0:T(8,128)(2,1)S(1)} %copy-done.56), channel_id=1, source_target_pairs={{0,4},{2,6},{4,0},{6,2},{8,12},{10,14},{12,8},{14,10},{16,20},{18,... | collective-permute-start | bytes 1572872 | tf_op jit(solution)/shard_map/ppermute | solution.py:33
  410.3 51.2 %collective-permute-start.26 = (f32[4,128,768]{2,1,0:T(8,128)}, f32[4,128,768]{2,1,0:T(8,128)}, u32[]{:S(2)}, u32[]{:S(2)}) collective-permute-start(f32[4,128,768]{2,1,0:T(8,128)} %get-tuple-element.85), channel_id=1, source_target_pairs={{0,6},{2,0},{4,2},{6,4},{8,14},{10,8},{12,10},{14,12},{16,22},{18,... | collective-permute-start | bytes 4718600 | tf_op jit(solution)/shard_map/ppermute | solution.py:33
  416.9 49.9 %collective-permute-start.25 = (f32[4,128,768]{2,1,0:T(8,128)S(1)}, f32[4,128,768]{2,1,0:T(8,128)}, u32[]{:S(2)}, u32[]{:S(2)}) collective-permute-start(f32[4,128,768]{2,1,0:T(8,128)S(1)} %get-tuple-element.84), channel_id=1, source_target_pairs={{0,2},{2,4},{4,6},{6,0},{8,10},{10,12},{12,14},{14,8},{16,18},{18,... | collective-permute-start | bytes 4718600 | tf_op jit(solution)/shard_map/ppermute | solution.py:33
  426.8 40.0 %collective-permute-start.48 = (f32[4,128,512]{2,1,0:T(8,128)S(1)}, f32[4,128,512]{2,1,0:T(8,128)S(1)}, u32[]{:S(2)}, u32[]{:S(2)}) collective-permute-start(f32[4,128,512]{2,1,0:T(8,128)S(1)} %get-tuple-element.94), channel_id=1, source_target_pairs={{0,16},{2,18},{4,20},{6,22},{8,24},{10,26},{12,28},{14,30},{16,0},... | collective-permute-start | bytes 3145736 | tf_op jit(solution)/shard_map/ppermute | solution.py:33
  428.9 41.1 %collective-permute-start.47 = (f32[4,128,512]{2,1,0:T(8,128)S(1)}, f32[4,128,512]{2,1,0:T(8,128)S(1)}, u32[]{:S(2)}, u32[]{:S(2)}) collective-permute-start(f32[4,128,512]{2,1,0:T(8,128)S(1)} %get-tuple-element.93), channel_id=1, source_target_pairs={{0,24},{2,26},{4,28},{6,30},{8,0},{10,2},{12,4},{14,6},{16,8},{18,... | collective-permute-start | bytes 3145736 | tf_op jit(solution)/shard_map/ppermute | solution.py:33
  436.6 77.0 %collective-permute-start.3 = (bf16[512,2048]{1,0:T(8,128)(2,1)S(1)}, bf16[512,2048]{1,0:T(8,128)(2,1)S(1)}, u32[]{:S(2)}, u32[]{:S(2)}) collective-permute-start(bf16[512,2048]{1,0:T(8,128)(2,1)S(1)} %add_convert_fusion), channel_id=1, source_target_pairs={{0,1},{1,0},{2,3},{3,2},{4,5},{5,4},{6,7},{7,6},{8,9},{9,8},{10,11... | collective-permute-start | bytes 6291464 | tf_op jit(solution)/shard_map/ppermute | solution.py:37
  466.8 41.8 %collective-permute-start.53 = (bf16[256,2048]{1,0:T(8,128)(2,1)S(1)}, bf16[256,2048]{1,0:T(8,128)(2,1)S(1)}, u32[]{:S(2)}, u32[]{:S(2)}) collective-permute-start(bf16[256,2048]{1,0:T(8,128)(2,1)S(1)} %constant_dynamic-slice_fusion.11), channel_id=1, source_target_pairs={{0,96},{2,98},{4,100},{6,102},{8,104},{10,106},{12,108},{14,110},{... | collective-permute-start | bytes 3145736 | tf_op jit(solution)/shard_map/ppermute | solution.py:33
  470.0 40.4 %collective-permute-start.54 = (bf16[256,2048]{1,0:T(8,128)(2,1)S(1)}, bf16[256,2048]{1,0:T(8,128)(2,1)S(1)}, u32[]{:S(2)}, u32[]{:S(2)}) collective-permute-start(bf16[256,2048]{1,0:T(8,128)(2,1)S(1)} %constant_dynamic-slice_fusion.11), channel_id=1, source_target_pairs={{0,64},{2,66},{4,68},{6,70},{8,72},{10,74},{12,76},{14,78},{16,80}... | collective-permute-start | bytes 3145736 | tf_op jit(solution)/shard_map/ppermute | solution.py:33
  481.8 54.8 %collective-permute-start.1 = (bf16[512,2048]{1,0:T(8,128)(2,1)}, bf16[512,2048]{1,0:T(8,128)(2,1)}, u32[]{:S(2)}, u32[]{:S(2)}) collective-permute-start(bf16[512,2048]{1,0:T(8,128)(2,1)} %convolution_convert_fusion.3), channel_id=1, source_target_pairs={{0,1},{1,0},{2,3},{3,2},{4,5},{5,4},{6,7},{7,6},{8,9},{9,8},{10,11... | collective-permute-start | bytes 6291464 | tf_op jit(solution)/shard_map/ppermute | solution.py:37
  (117 other events, 2192.6 us)
where the time goes:
time: 643 us; the launch traced here: 634 us
  waiting for transfers between devices  240 us (37%)
  Pallas kernels  124 us (19%)
  matrix products  101 us (16%)
  starting transfers between devices  68.4 us (11%)
  other arithmetic  50.4 us (8%)
  local copies, waits for them, and re-layouts  46.6 us (7%)
    ppermute x45, waiting for transfers between devices, shift(): return lax.ppermute(values, 'dp', pairs)  240 us
    ppermute x45, starting transfers between devices, shift(): return lax.ppermute(values, 'dp', pairs)  65.8 us
    dot_general x7, matrix products, project(): jnp.einsum('...d,df->...f', values, weight, preferred_element_type=jnp.fl...  52.8 us
    dot_general x7, matrix products, project_back(): jnp.einsum('...f,df->...d', grads, weight, preferred_element_type=jnp.flo...  48.5 us
    pallas_call x2, Pallas kernels, exchange(): pl.pallas_call(functools.partial(exchange_kernel, [offset for _, offset,...  47.4 us
    pallas_call x3, Pallas kernels, column_parts(): pl.pallas_call(functools.partial(column_kernel, hi_mode, width, n_chunks)...  36.5 us
    unnamed x191, local copies, waits for them, and re-layouts  22.3 us
    pallas_call x2, Pallas kernels, attention_call(): pl.pallas_call(body, grid=(n_rows, kv_heads), in_specs=[pl.BlockSpec((1,...  21.1 us
  transfers between devices with their start and end apart: 61, of which 19 were waited for; matrix products, arithmetic and copies ran while one was open for 25% of the time, Pallas kernels for 12%

commit v1 on v0

--- a/solution.py
+++ b/solution.py
@@ -69,24 +69,30 @@
     return parts[0] + parts[1] + parts[2] + parts[3]
 
 
-def exchange_kernel(routes, *refs):
-    n = len(routes)
-    sources, targets, (send_sem, recv_sem) = refs[:n], refs[n:2 * n], refs[2 * n:]
+def exchange_kernel(entries, n_in, n_out, *refs):
+    sources, targets, (send_sem, recv_sem) = refs[:n_in], refs[n_in:n_in + n_out], refs[n_in + n_out:]
     chip = lax.axis_index("dp")
 
     def chip_at(offset, sign):
         return to_chip(chip, **{a: coord_of(chip, a) + sign * offset[k] + 4 for k, a in enumerate("zyx")})
 
     barrier = pltpu.get_barrier_semaphore()
-    offsets = sorted(set(routes))
+    offsets = sorted({entry[0] for entry in entries if any(entry[0])})
     for offset in offsets:
         pl.semaphore_signal(barrier, inc=1, device_id={"dp": chip_at(offset, -1)}, device_id_type=pl.DeviceIdType.MESH)
     pl.semaphore_wait(barrier, len(offsets))
+    here = {a: coord_of(chip, a) for a in "zyx"}
     copies = []
-    for k, offset in enumerate(routes):
-        copies.append(pltpu.make_async_remote_copy(
-            src_ref=sources[k], dst_ref=targets[k], send_sem=send_sem.at[k], recv_sem=recv_sem.at[k],
-            device_id={"dp": chip_at(offset, 1)}, device_id_type=pl.DeviceIdType.MESH))
+    for k, (offset, source, view, target, place) in enumerate(entries):
+        peer = chip_at(offset, 1)
+        there = {a: coord_of(peer, a) for a in "zyx"}
+        src, dst = view(sources[source], there), place(targets[target], here)
+        if any(offset):
+            copies.append(pltpu.make_async_remote_copy(
+                src_ref=src, dst_ref=dst, send_sem=send_sem.at[k], recv_sem=recv_sem.at[k],
+                device_id={"dp": peer}, device_id_type=pl.DeviceIdType.MESH))
+        else:
+            copies.append(pltpu.make_async_copy(src, dst, send_sem.at[k]))
     for copy in copies:
         copy.start()
     for copy in copies:
@@ -97,40 +103,51 @@
     return [tuple(d if a == axis else 0 for a in "zyx") for d in (2, 1, 3)]
 
 
-def exchange(groups, call_id):
-    entries = [(g, offset, value) for g, group in enumerate(groups) for offset, value in group]
-    values = [value for _, _, value in entries]
-    any_spec = pl.BlockSpec(memory_space=pl.ANY)
-    n = len(values)
-    sent = sum(v.size * v.dtype.itemsize for v in values)
-    out = pl.pallas_call(
-        functools.partial(exchange_kernel, [offset for _, offset, _ in entries]),
-        in_specs=[any_spec] * n,
-        out_specs=[any_spec] * n,
-        out_shape=[jax.ShapeDtypeStruct(v.shape, v.dtype) for v in values],
-        scratch_shapes=[pltpu.SemaphoreType.DMA((n,)), pltpu.SemaphoreType.DMA((n,))],
-        compiler_params=pltpu.CompilerParams(collective_id=call_id, has_side_effects=True),
-        cost_estimate=pl.CostEstimate(flops=0, bytes_accessed=2 * sent, transcendentals=0),
-    )(*values)
-    out = lax.optimization_barrier(out)
-    got = [{} for _ in groups]
-    for (g, offset, _), value in zip(entries, out):
-        got[g][offset] = value
-    return got
-
-
-def line_group(axis, turn):
-    return [(offset, turn[sum(offset)]) for offset in along(axis)]
-
-
-def line_values(got):
-    by_distance = {sum(offset): value for offset, value in got.items()}
-    return [by_distance[d] for d in (1, 2, 3)]
-
-
-def in_source_order(own, received, here):
-    stacked = jnp.stack([own] + received)
-    return [pick(stacked, here - b, 0) for b in range(4)]
+HERE = (0, 0, 0)
+
+
+class Exchange:
+    def __init__(self):
+        self.values, self.shapes, self.entries = [], [], []
+
+    def add(self, value, shape, offsets, view, place):
+        self.values.append(value)
+        self.shapes.append(shape)
+        for offset in offsets:
+            self.entries.append((offset, len(self.values) - 1, view, len(self.shapes) - 1, place(offset)))
+        return len(self.shapes) - 1
+
+    def line_sum(self, value, axis):
+        return self.add(value, (3,) + value.shape[1:], along(axis), lambda ref, there: ref.at[there[axis]],
+                        lambda offset: lambda ref, here: ref.at[sum(offset) - 1])
+
+    def line_parts(self, parts, axis):
+        for offset in along(axis):
+            self.add(parts[sum(offset)], parts[0].shape, [offset], lambda ref, there: ref, lambda offset: lambda ref, here: ref)
+
+    def line_columns(self, value, axis, first, width):
+        return self.add(value, (value.shape[1], 4 * width), along(axis) + [HERE],
+                        lambda ref, there: ref.at[there[axis], :, pl.ds(first, width)],
+                        lambda offset: lambda ref, here: ref.at[:, pl.ds(pl.multiple_of(here[axis] * width, 128), width)])
+
+    def to_all(self, value, offsets, slots, slot_of):
+        return self.add(value, (slots,) + value.shape, offsets + [HERE], lambda ref, there: ref,
+                        lambda offset: lambda ref, here: ref.at[slot_of(here)])
+
+    def run(self, call_id):
+        any_spec = pl.BlockSpec(memory_space=pl.ANY)
+        n = len(self.entries)
+        sent = sum(v.size * v.dtype.itemsize for v in self.values)
+        out = pl.pallas_call(
+            functools.partial(exchange_kernel, self.entries, len(self.values), len(self.shapes)),
+            in_specs=[any_spec] * len(self.values),
+            out_specs=[any_spec] * len(self.shapes),
+            out_shape=[jax.ShapeDtypeStruct(shape, jnp.float32) for shape in self.shapes],
+            scratch_shapes=[pltpu.SemaphoreType.DMA((n,)), pltpu.SemaphoreType.DMA((n,))],
+            compiler_params=pltpu.CompilerParams(collective_id=call_id, has_side_effects=True),
+            cost_estimate=pl.CostEstimate(flops=0, bytes_accessed=2 * sent, transcendentals=0),
+        )(*self.values)
+        return lax.optimization_barrier(out)
 
 
 def load_plan(own_rows, shared):
@@ -494,45 +511,40 @@
     up_parts = column_parts(mlp_in_y, d_up_all, d_up.shape[-1] // 4, info("z", "x", "y"), False, 4)
     up_sent = [shift(up_parts[d], "x", d) for d in STEPS]
     out_parts = row_parts(context_all, d_hidden_all, context.shape[-1] // 4, info("x", "x", "z"), True, False)
-    out_sent = [shift(out_parts[d], "x", d) for d in STEPS]
     qkv_parts = column_parts(attn_in_all, qkv_all, qkv_all[1].shape[1], info("z", "y", "x"), False, 1)
     qkv_sent = [shift(qkv_parts[d], "y", d) for d in STEPS]
     g_down = add_parts([down_parts[0]] + down_sent).reshape(4, -1, width)
     g_gate = add_parts([gate_parts[0]] + gate_sent).reshape(4, 128, -1)
     g_up = add_parts([up_parts[0]] + up_sent)
-    g_out = add_parts([out_parts[0]] + out_sent)
     g_qkv = add_parts([qkv_parts[0]] + qkv_sent)
 
-    def turns(values, here, dim=0):
-        return [pick(values, here + d, dim) for d in range(4)]
-
-    gate_turn, up_turn, down_turn = turns(g_gate, at["y"]), turns(g_up, at["z"]), turns(g_down, at["x"])
-    qkv_turn, out_turn = turns(g_qkv, at["z"]), turns(g_out, at["y"])
-    got = exchange([
-        line_group("y", gate_turn), line_group("z", up_turn), line_group("x", down_turn), line_group("z", qkv_turn),
-        line_group("y", out_turn), line_group("x", [gains] * 4),
-    ], 1)
-    got = [line_values(g) for g in got]
-    grad_down = add_parts([down_turn[0]] + got[2])
-    grad_out_w = add_parts([out_turn[0]] + got[4])
-    gains = add_parts(in_source_order(gains, got[5], at["x"]))
-    gate_turn = turns(add_parts([gate_turn[0]] + got[0]).reshape(4, n_own, -1), at["x"])
-    up_turn = turns(add_parts([up_turn[0]] + got[1]).reshape(4, n_own, -1), at["y"])
-    qkv_turn = turns(add_parts([qkv_turn[0]] + got[3]).reshape(4, n_own, -1), at["x"])
+    def line_total(value, here, got):
+        return pick(value, here, 0) + got[0] + got[1] + got[2]
+
+    first = Exchange()
+    first.line_sum(g_gate, "y"), first.line_sum(g_up, "z"), first.line_parts(out_parts, "x")
+    got = first.run(1)
+    g_gate = line_total(g_gate, at["y"], got[0]).reshape(4, n_own, -1)
+    g_up = line_total(g_up, at["z"], got[1]).reshape(4, n_own, -1)
+    g_out = add_parts([out_parts[0]] + list(got[2:5]))
+    second = Exchange()
+    second.line_sum(g_qkv, "z"), second.line_sum(g_out, "y")
+    second.line_columns(g_gate, "x", 0, g_gate.shape[2]), second.line_columns(g_up, "y", 0, g_up.shape[2])
+    second.to_all(gains, along("x"), 4, lambda here: here["x"])
+    second.line_sum(g_down, "x")
+    got = second.run(2)
+    g_qkv = line_total(g_qkv, at["z"], got[0]).reshape(4, n_own, -1)
+    grad_out_w = line_total(g_out, at["y"], got[1])
+    grad_gate, grad_up = got[2], got[3]
+    gains = jnp.sum(got[4], axis=0)
+    grad_down = line_total(g_down, at["x"], got[5])
+    third = Exchange()
+    third.line_columns(g_qkv, "x", 0, n_q), third.line_columns(g_qkv, "x", n_q, n_k), third.line_columns(g_qkv, "x", n_q + n_k, n_k)
     plane = [(dz, dy, 0) for dz in range(4) for dy in range(4) if dz or dy]
-    got = exchange([
-        line_group("x", gate_turn), line_group("y", up_turn), line_group("x", qkv_turn), [(offset, gains) for offset in plane],
-    ], 2)
-    grad_gate = jnp.concatenate(in_source_order(gate_turn[0], line_values(got[0]), at["x"]), axis=1)
-    grad_up = jnp.concatenate(in_source_order(up_turn[0], line_values(got[1]), at["y"]), axis=1)
-    ordered = in_source_order(qkv_turn[0], line_values(got[2]), at["x"])
-    in_plane = jnp.stack([got[3].get((dz, dy, 0), gains) for dz in range(4) for dy in range(4)]).reshape(4, 4, 2, width)
-    in_plane = jnp.stack([pick(in_plane, at["z"] - z, 0) for z in range(4)])
-    in_plane = jnp.stack([pick(in_plane, at["y"] - y, 1) for y in range(4)])
-    gains = jnp.sum(in_plane, axis=(0, 1))
-    grad_query = jnp.concatenate([o[:, :n_q] for o in ordered], axis=1)
-    grad_key = jnp.concatenate([o[:, n_q:n_q + n_k] for o in ordered], axis=1)
-    grad_value = jnp.concatenate([o[:, n_q + n_k:] for o in ordered], axis=1)
+    third.to_all(gains, plane, 16, lambda here: 4 * here["z"] + here["y"])
+    got = third.run(3)
+    grad_query, grad_key, grad_value = got[:3]
+    gains = jnp.sum(got[3], axis=0)
     return (
         layer_out,
         grad_tokens,

time: 643 us -> 647 us (level)
  waiting for transfers between devices: 240 us -> 155 us
  starting transfers between devices: 68.4 us -> 124 us
  Pallas kernels: 124 us -> 152 us
  other arithmetic: 50.4 us -> 62 us
  local copies, waits for them, and re-layouts: 46.6 us -> 36.1 us
  matrix products: 101 us -> 110 us
    ppermute x45 -> x42, waiting for transfers between devices: 240 us -> 155 us  [shift(): return lax.ppermute(values, 'dp', pairs)]
    ppermute x45 -> x42, starting transfers between devices: 65.8 us -> 121 us  [shift(): return lax.ppermute(values, 'dp', pairs)]
    pallas_call x2 -> x3, Pallas kernels: 47.4 us -> 71.3 us  [run(): pl.pallas_call(functools.partial(exchange_kernel, self.entries, len(self....]
    add x0 -> x4, other arithmetic: none -> 8.13 us  [line_total(): return pick(value, here, 0) + got[0] + got[1] + got[2]]
    dot_general x7, matrix products: 48.5 us -> 55.1 us  [project_back(): jnp.einsum('...f,df->...d', grads, weight, preferred_element_type=jnp.flo...]
    unnamed x191 -> x156, local copies, waits for them, and re-layouts: 22.3 us -> 20.1 us
    add x10 -> x5, other arithmetic: 15 us -> 15.1 us  [add_parts(): return parts[0] + parts[1] + parts[2] + parts[3]]
  transfers between devices with their start and end apart: 61 -> 58, of which waited for: 19 -> 15; matrix products, arithmetic and copies ran while one was open for 25% -> 26% of each run, Pallas kernels for 12% -> 11%
where the time goes in v1:
time: 647 us; the launch traced here: 640 us
  waiting for transfers between devices  155 us (24%)
  Pallas kernels  152 us (23%)
  starting transfers between devices  124 us (19%)
  matrix products  110 us (17%)
  other arithmetic  62 us (10%)
  local copies, waits for them, and re-layouts  36.1 us (6%)
    ppermute x42, waiting for transfers between devices, shift(): return lax.ppermute(values, 'dp', pairs)  155 us
    ppermute x42, starting transfers between devices, shift(): return lax.ppermute(values, 'dp', pairs)  121 us
    pallas_call x3, Pallas kernels, run(): pl.pallas_call(functools.partial(exchange_kernel, self.entries, len(self....  71.3 us
    dot_general x7, matrix products, project_back(): jnp.einsum('...f,df->...d', grads, weight, preferred_element_type=jnp.flo...  55.1 us
    dot_general x7, matrix products, project(): jnp.einsum('...d,df->...f', values, weight, preferred_element_type=jnp.fl...  54.5 us
    pallas_call x3, Pallas kernels, column_parts(): pl.pallas_call(functools.partial(column_kernel, hi_mode, width, n_chunks)...  39.8 us
    pallas_call x2, Pallas kernels, attention_call(): pl.pallas_call(body, grid=(n_rows, kv_heads), in_specs=[pl.BlockSpec((1,...  21.1 us
    unnamed x156, local copies, waits for them, and re-layouts  20.1 us
  transfers between devices with their start and end apart: 58, of which 15 were waited for; matrix products, arithmetic and copies ran while one was open for 26% of the time, Pallas kernels for 11%

profile of v1, /device:TPU:0, one launch (start us, length us, event | category | flops | bytes accessed | tf_op | source)
XLA Modules:
  0.0 640.2 jit_solution(10408898173364496380)
XLA Ops:
  15.4 6.3 convolution_convert_fusion.6.query_ref
  25.8 9.5 %shard_map.203.refs_0_ = bf16[512,1024]{1,0:T(8,128)(2,1)} custom-call(s32[2,256,1]{2,1,0:T(8,128)} %copy.23.seg_col_ref, s32[2,1,256]{2,1,0:T(1,128)} %broadcast_in_dim.9.seg_row_ref, bf16[512,1024]{1,0:T(8,128)(2,1)} %convolution_convert_fusion.6.query_ref, bf16[512,512]{1,0:T(8,128)(2,1)} %convolution_convert_fusion.8.key_ref, ...), custom_call_target="tpu_custom_call" | custom-call | flops 2147483648 | bytes 8388608 | tf_op jit(solution)/shard_map/pallas_call | solution.py:424
  35.3 6.2 convolution_convert_fusion.4
  41.5 13.3 %collective-permute-start.52 = (bf16[512,2048]{1,0:T(8,128)(2,1)}, bf16[512,2048]{1,0:T(8,128)(2,1)}, u32[]{:S(2)}, u32[]{:S(2)}) collective-permute-start(bf16[512,2048]{1,0:T(8,128)(2,1)} %bitcast.3.refs_4_), channel_id=1, source_target_pairs={{0,32},{2,34},{4,36},{6,38},{8,40},{10,42},{12,44},{14,46},{16,48}... | collective-permute-start | bytes 6291464 | tf_op jit(solution)/shard_map/ppermute | solution.py:33
  56.3 13.1 %convolution_convert_fusion = bf16[512,3072]{1,0:T(8,128)(2,1)} fusion(bf16[512,2048]{1,0:T(8,128)(2,1)} %bitcast.3.refs_4_, bf16[3072,2048]{1,0:T(8,128)(2,1)} %param.23), kind=kOutput, calls=%fused_computation.24 | convolution fusion | flops 6444023808 | bytes 17825792 | tf_op jit(solution)/shard_map/...f,df->...d/dot_general | solution.py:441
  76.3 10.6 %convolution_convert_fusion.1 = bf16[512,3072]{1,0:T(8,128)(2,1)S(1)} fusion(bf16[512,2048]{1,0:T(8,128)(2,1)S(1)} %fusion.10.refs_0_, bf16[2048,3072]{1,0:T(8,128)(2,1)} %param.22), kind=kOutput, calls=%fused_computation.25 | convolution fusion | flops 6444023808 | bytes 17825792 | tf_op jit(solution)/shard_map/...d,df->...f/dot_general | solution.py:437
  86.9 16.5 %fusion.1 = (bf16[512,3072]{1,0:T(8,128)(2,1)S(1)}, bf16[512,3072]{1,0:T(8,128)(2,1)S(1)}, bf16[512,3072]{1,0:T(8,128)(2,1)}) fusion(bf16[512,3072]{1,0:T(8,128)(2,1)} %convolution_convert_fusion, bf16[512,3072]{1,0:T(8,128)(2,1)S(1)} %convolution_convert_fusion.1, bf16[512,2048]{1,0:T(8,128)(2,1)S(1)} %fusion.10.refs_0_, bf16[2048,3072]{1,0:T(8,128)(2,1)} %param.21), kind=kOutput, calls=%fused_computation.13 | convolution fusion | flops 6473908224 | bytes 30408704 | tf_op jit(solution)/shard_map/...d,df->...f/dot_general | solution.py:437
  107.5 11.0 %fusion.29 = f32[512,2048]{1,0:T(8,128)} fusion(bf16[512,3072]{1,0:T(8,128)(2,1)S(1)} %get-tuple-element.94.refs_7_, bf16[2048,3072]{1,0:T(8,128)(2,1)} %param.21), kind=kOutput, calls=%fused_computation.110 | convolution fusion | flops 6442450944 | bytes 19922944 | tf_op jit(solution)/shard_map/...f,df->...d/dot_general | solution.py:441
  127.1 13.6 %add_convert_fusion.1 = bf16[512,2048]{1,0:T(8,128)(2,1)} fusion(f32[512,2048]{1,0:T(8,128)} %fusion.29, bf16[512,3072]{1,0:T(8,128)(2,1)} %copy-done.8, bf16[2048,3072]{1,0:T(8,128)(2,1)} %param.22), kind=kOutput, calls=%fused_computation.50 | convolution fusion | flops 6444548096 | bytes 22020096 | tf_op jit(solution)/shard_map/...f,df->...d/dot_general | solution.py:441
  143.7 24.5 %collective-permute-done.54.refs_7_ = bf16[512,2048]{1,0:T(8,128)(2,1)} collective-permute-done((bf16[512,2048]{1,0:T(8,128)(2,1)}, bf16[512,2048]{1,0:T(8,128)(2,1)}, u32[]{:S(2)}, u32[]{:S(2)}) %collective-permute-start.54) | collective-permute-done | bytes 2097184 | tf_op jit(solution)/shard_map/ppermute | solution.py:33
  172.5 10.7 %convolution_convert_fusion.3 = bf16[512,2048]{1,0:T(8,128)(2,1)} fusion(bf16[512,3072]{1,0:T(8,128)(2,1)S(1)} %copy-done.46, bf16[3072,2048]{1,0:T(8,128)(2,1)} %param.23), kind=kOutput, calls=%fused_computation.51 | convolution fusion | flops 6443499520 | bytes 17825792 | tf_op jit(solution)/shard_map/...d,df->...f/dot_general | solution.py:437
  183.2 7.1 %collective-permute-done.49.refs_1_ = bf16[512,768]{1,0:T(8,128)(2,1)S(1)} collective-permute-done((bf16[512,768]{1,0:T(8,128)(2,1)S(1)}, bf16[512,768]{1,0:T(8,128)(2,1)S(1)}, u32[]{:S(2)}, u32[]{:S(2)}) %collective-permute-start.49) | collective-permute-done | bytes 786464 | tf_op jit(solution)/shard_map/ppermute | solution.py:33
  193.0 12.8 %collective-permute-done.50.refs_2_ = bf16[512,768]{1,0:T(8,128)(2,1)S(1)} collective-permute-done((bf16[512,768]{1,0:T(8,128)(2,1)S(1)}, bf16[512,768]{1,0:T(8,128)(2,1)S(1)}, u32[]{:S(2)}, u32[]{:S(2)}) %collective-permute-start.50) | collective-permute-done | bytes 786464 | tf_op jit(solution)/shard_map/ppermute | solution.py:33
  209.4 11.6 %shard_map.210 = (f32[192,2048]{1,0:T(8,128)S(1)}, f32[192,2048]{1,0:T(8,128)S(1)}, f32[192,2048]{1,0:T(8,128)}, f32[192,2048]{1,0:T(8,128)}) custom-call(s32[4]{0:T(128)S(1)} %add_add_fusion.10.info, bf16[512,3072]{1,0:T(8,128)(2,1)} %get-tuple-element.95.refs_0_, bf16[512,768]{1,0:T(8,128)(2,1)S(1)} %collective-permute-done.49.refs_1_, ...), custom_call_target="tpu_custom_call" | custom-call | flops 6442450944 | bytes 20971520 | tf_op jit(solution)/shard_map/pallas_call | solution.py:349
  229.1 8.0 %collective-permute-done.26.refs_2_ = bf16[256,2048]{1,0:T(8,128)(2,1)S(1)} collective-permute-done((bf16[256,2048]{1,0:T(8,128)(2,1)}, bf16[256,2048]{1,0:T(8,128)(2,1)S(1)}, u32[]{:S(2)}, u32[]{:S(2)}) %collective-permute-start.26) | collective-permute-done | bytes 1048608 | tf_op jit(solution)/shard_map/ppermute | solution.py:33
  247.5 19.7 %collective-permute-start.44 = (bf16[512,768]{1,0:T(8,128)(2,1)S(1)}, bf16[512,768]{1,0:T(8,128)(2,1)S(1)}, u32[]{:S(2)}, u32[]{:S(2)}) collective-permute-start(bf16[512,768]{1,0:T(8,128)(2,1)S(1)} %copy-done.58), channel_id=1, source_target_pairs={{0,24},{2,26},{4,28},{6,30},{8,0},{10,2},{12,4},{14,6},{16,8},{18,... | collective-permute-start | bytes 2359304 | tf_op jit(solution)/shard_map/ppermute | solution.py:33
  271.3 11.5 %shard_map.207 = (f32[512,768]{1,0:T(8,128)S(1)}, f32[512,768]{1,0:T(8,128)S(1)}, f32[512,768]{1,0:T(8,128)S(1)}, f32[512,768]{1,0:T(8,128)S(1)}) custom-call(s32[4]{0:T(128)S(1)} %add_add_fusion.7.info, bf16[512,2048]{1,0:T(8,128)(2,1)S(1)} %fusion.10.refs_0_, bf16[256,2048]{1,0:T(8,128)(2,1)S(1)} %collective-permute-done.25.refs_1_, ...), custom_call_target="tpu_custom_call" | custom-call | flops 6442450944 | bytes 20971520 | tf_op jit(solution)/shard_map/pallas_call | solution.py:255
  292.8 29.5 %collective-permute-start.56 = (f32[192,2048]{1,0:T(8,128)}, f32[192,2048]{1,0:T(8,128)}, u32[]{:S(2)}, u32[]{:S(2)}) collective-permute-start(f32[192,2048]{1,0:T(8,128)} %get-tuple-element.75), channel_id=1, source_target_pairs={{0,24},{2,26},{4,28},{6,30},{8,0},{10,2},{12,4},{14,6},{16,8},{18,... | collective-permute-start | bytes 4718600 | tf_op jit(solution)/shard_map/ppermute | solution.py:33
  322.3 11.6 %shard_map.204 = (bf16[512,1024]{1,0:T(8,128)(2,1)}, bf16[512,512]{1,0:T(8,128)(2,1)}, bf16[512,512]{1,0:T(8,128)(2,1)}) custom-call(s32[2,256,1]{2,1,0:T(8,128)} %copy.23.seg_col_ref, s32[2,1,256]{2,1,0:T(1,128)} %broadcast_in_dim.9.seg_row_ref, bf16[512,1024]{1,0:T(8,128)(2,1)} %convolution_convert_fusion.6.query_ref, ...), custom_call_target="tpu_custom_call" | custom-call | flops 5368709120 | bytes 8388608 | tf_op jit(solution)/shard_map/pallas_call | solution.py:424
  344.4 19.7 %shard_map.208 = (f32[4,128,768]{2,1,0:T(8,128)S(1)}, f32[4,128,768]{2,1,0:T(8,128)S(1)}, f32[4,128,768]{2,1,0:T(8,128)S(1)}, f32[4,128,768]{2,1,0:T(8,128)S(1)}) custom-call(s32[4]{0:T(128)S(1)} %add_add_fusion.9.info, bf16[512,2048]{1,0:T(8,128)(2,1)S(1)} %copy-done.6, bf16[256,2048]{1,0:T(8,128)(2,1)} %collective-permute-done.37.refs_1_, ...), custom_call_target="tpu_custom_call" | custom-call | flops 6442450944 | bytes 20971520 | tf_op jit(solution)/shard_map/pallas_call | solution.py:255
  383.9 6.2 collective-permute-done.11.refs_9_
  400.1 6.3 add_convert_fusion
  413.9 8.6 %shard_map.205 = (f32[4,128,512]{2,1,0:T(8,128)S(1)}, f32[4,128,512]{2,1,0:T(8,128)S(1)}, f32[4,128,512]{2,1,0:T(8,128)S(1)}, f32[4,128,512]{2,1,0:T(8,128)S(1)}) custom-call(s32[4]{0:T(128)S(1)} %add_add_fusion.7.info, bf16[512,2048]{1,0:T(8,128)(2,1)S(1)} %copy-done.4, bf16[256,2048]{1,0:T(8,128)(2,1)} %collective-permute-done.4.refs_1_, ...), custom_call_target="tpu_custom_call" | custom-call | flops 4294967296 | bytes 20971520 | tf_op jit(solution)/shard_map/pallas_call | solution.py:255
  423.0 5.9 collective-permute-done.48
  431.1 30.5 %collective-permute-done.47 = f32[4,128,768]{2,1,0:T(8,128)} collective-permute-done((f32[4,128,768]{2,1,0:T(8,128)S(1)}, f32[4,128,768]{2,1,0:T(8,128)}, u32[]{:S(2)}, u32[]{:S(2)}) %collective-permute-start.47) | collective-permute-done | bytes 1572896 | tf_op jit(solution)/shard_map/ppermute | solution.py:33
  475.5 9.8 %collective-permute-done.14 = f32[4,128,512]{2,1,0:T(8,128)S(1)} collective-permute-done((f32[4,128,512]{2,1,0:T(8,128)S(1)}, f32[4,128,512]{2,1,0:T(8,128)S(1)}, u32[]{:S(2)}, u32[]{:S(2)}) %collective-permute-start.14) | collective-permute-done | bytes 1048608 | tf_op jit(solution)/shard_map/ppermute | solution.py:33
  494.6 33.0 %collective-permute-done.16.refs_1_ = bf16[512,256]{1,0:T(8,128)(2,1)S(1)} collective-permute-done((bf16[512,256]{1,0:T(8,128)(2,1)S(1)}, bf16[512,256]{1,0:T(8,128)(2,1)S(1)}, u32[]{:S(2)}, u32[]{:S(2)}) %collective-permute-start.16) | collective-permute-done | bytes 262176 | tf_op jit(solution)/shard_map/ppermute | solution.py:33
  529.7 9.2 %fusion.14 = (bf16[512,2048]{1,0:T(8,128)(2,1)}, bf16[512,2048]{1,0:T(8,128)(2,1)}) fusion(bf16[2,256,2048]{2,1,0:T(8,128)(2,1)S(1)} %copy-done.37, bf16[512,2048]{1,0:T(8,128)(2,1)} %collective-permute-done.3, bf16[512,2048]{1,0:T(8,128)(2,1)} %add_convert_fusion, f32[512]{0:T(512)S(1)} %multiply_multiply_fusion, f32[2048]{0:T(1024)S(1)} %copy-done.65, ...), kind=kLoop, calls=%fused_computation.31 | loop fusion | flops 31457280 | bytes 23093248 | tf_op jit(solution)/shard_map/convert_element_type | solution.py:504
  539.5 7.8 %shard_map.206 = (f32[4,16,2048]{2,1,0:T(8,128)S(1)}, f32[4,16,2048]{2,1,0:T(8,128)S(1)}, f32[4,16,2048]{2,1,0:T(8,128)S(1)}, f32[4,16,2048]{2,1,0:T(8,128)S(1)}) custom-call(s32[4]{0:T(128)S(1)} %add_add_fusion.8.info, bf16[512,1024]{1,0:T(8,128)(2,1)S(1)} %copy-done.7, bf16[512,256]{1,0:T(8,128)(2,1)S(1)} %collective-permute-done.16.refs_1_, ...), custom_call_target="tpu_custom_call" | custom-call | flops 2147483648 | bytes 20971520 | tf_op jit(solution)/shard_map/pallas_call | solution.py:349
  550.6 33.0 %shard_map.209 = (f32[3,128,768]{2,1,0:T(8,128)}, f32[3,128,768]{2,1,0:T(8,128)}, f32[4,16,2048]{2,1,0:T(8,128)}, f32[4,16,2048]{2,1,0:T(8,128)}, f32[4,16,2048]{2,1,0:T(8,128)}) custom-call(f32[4,128,768]{2,1,0:T(8,128)} %bitcast.79, f32[4,128,768]{2,1,0:T(8,128)} %add_add_fusion.3.refs_1_, f32[4,16,2048]{2,1,0:T(8,128)} %copy-done.19, ...), custom_call_target="tpu_custom_call" | custom-call | bytes 9437184 | tf_op jit(solution)/shard_map/pallas_call | solution.py:141
  588.2 27.6 %shard_map.211 = (f32[3,128,512]{2,1,0:T(8,128)}, f32[3,16,2048]{2,1,0:T(8,128)}, f32[32,3072]{1,0:T(8,128)}, f32[32,3072]{1,0:T(8,128)}, f32[4,2,2048]{2,1,0:T(2,128)}, /*index=5*/f32[3,48,2048]{2,1,0:T(8,128)}) custom-call(f32[4,128,512]{2,1,0:T(8,128)} %add_add_fusion.5.refs_0_, f32[4,16,2048]{2,1,0:T(8,128)} %add_add_fusion.6.refs_1_, ...), custom_call_target="tpu_custom_call" | custom-call | bytes 7897088 | tf_op jit(solution)/shard_map/pallas_call | solution.py:141
  619.4 10.6 %shard_map.212 = (f32[32,1024]{1,0:T(8,128)}, f32[32,512]{1,0:T(8,128)}, f32[32,512]{1,0:T(8,128)}, f32[16,2,2048]{2,1,0:T(2,128)}) custom-call(f32[4,32,512]{2,1,0:T(8,128)} %bitcast.81, f32[4,32,512]{2,1,0:T(8,128)} %bitcast.82, f32[4,32,512]{2,1,0:T(8,128)} %bitcast.83, f32[2,2048]{1,0:T(2,128)} %reduce_sum.79.refs_3_), custom_call_target="tpu_custom_call" | custom-call | bytes 1605632 | tf_op jit(solution)/shard_map/pallas_call | solution.py:141
  (309 shorter events, 182.6 us)
Async XLA Ops:
  8.8 60.7 %collective-permute-start.4 = (bf16[256,2048]{1,0:T(8,128)(2,1)}, bf16[256,2048]{1,0:T(8,128)(2,1)}, u32[]{:S(2)}, u32[]{:S(2)}) collective-permute-start(bf16[256,2048]{1,0:T(8,128)(2,1)} %constant_dynamic-slice_fusion.26), channel_id=1, source_target_pairs={{0,2},{2,4},{4,6},{6,0},{8,10},{10,12},{12,14},{14,8},{16,18},{18,... | collective-permute-start | bytes 3145736 | tf_op jit(solution)/shard_map/ppermute | solution.py:33
  10.4 61.3 %collective-permute-start.5 = (bf16[256,2048]{1,0:T(8,128)(2,1)}, bf16[256,2048]{1,0:T(8,128)(2,1)}, u32[]{:S(2)}, u32[]{:S(2)}) collective-permute-start(bf16[256,2048]{1,0:T(8,128)(2,1)} %constant_dynamic-slice_fusion.26), channel_id=1, source_target_pairs={{0,6},{2,0},{4,2},{6,4},{8,14},{10,8},{12,10},{14,12},{16,22},{18,... | collective-permute-start | bytes 3145736 | tf_op jit(solution)/shard_map/ppermute | solution.py:33
  12.0 106.6 %collective-permute-start.6 = (bf16[256,2048]{1,0:T(8,128)(2,1)}, bf16[256,2048]{1,0:T(8,128)(2,1)}, u32[]{:S(2)}, u32[]{:S(2)}) collective-permute-start(bf16[256,2048]{1,0:T(8,128)(2,1)} %constant_dynamic-slice_fusion.26), channel_id=1, source_target_pairs={{0,4},{2,6},{4,0},{6,2},{8,12},{10,14},{12,8},{14,10},{16,20},{18,... | collective-permute-start | bytes 3145736 | tf_op jit(solution)/shard_map/ppermute | solution.py:33
  41.5 83.5 %collective-permute-start.52 = (bf16[512,2048]{1,0:T(8,128)(2,1)}, bf16[512,2048]{1,0:T(8,128)(2,1)}, u32[]{:S(2)}, u32[]{:S(2)}) collective-permute-start(bf16[512,2048]{1,0:T(8,128)(2,1)} %bitcast.3.refs_4_), channel_id=1, source_target_pairs={{0,32},{2,34},{4,36},{6,38},{8,40},{10,42},{12,44},{14,46},{16,48}... | collective-permute-start | bytes 6291464 | tf_op jit(solution)/shard_map/ppermute | solution.py:33
  69.4 56.1 %collective-permute-start.53 = (bf16[512,2048]{1,0:T(8,128)(2,1)}, bf16[512,2048]{1,0:T(8,128)(2,1)}, u32[]{:S(2)}, u32[]{:S(2)}) collective-permute-start(bf16[512,2048]{1,0:T(8,128)(2,1)} %bitcast.3.refs_4_), channel_id=1, source_target_pairs={{0,96},{2,98},{4,100},{6,102},{8,104},{10,106},{12,108},{14,110},{... | collective-permute-start | bytes 6291464 | tf_op jit(solution)/shard_map/ppermute | solution.py:33
  71.6 48.8 %collective-permute-start.7 = (bf16[256,2048]{1,0:T(8,128)(2,1)}, bf16[256,2048]{1,0:T(8,128)(2,1)S(1)}, u32[]{:S(2)}, u32[]{:S(2)}) collective-permute-start(bf16[256,2048]{1,0:T(8,128)(2,1)} %collective-permute-done.4.refs_1_), channel_id=1, source_target_pairs={{0,1},{1,0},{2,3},{3,2},{4,5},{5,4},{6,7},{7,6},{8,9},{9,8},{10,11... | collective-permute-start | bytes 3145736 | tf_op jit(solution)/shard_map/ppermute | solution.py:37
  71.9 49.5 %collective-permute-start.8 = (bf16[256,2048]{1,0:T(8,128)(2,1)}, bf16[256,2048]{1,0:T(8,128)(2,1)S(1)}, u32[]{:S(2)}, u32[]{:S(2)}) collective-permute-start(bf16[256,2048]{1,0:T(8,128)(2,1)} %collective-permute-done.5.refs_2_), channel_id=1, source_target_pairs={{0,1},{1,0},{2,3},{3,2},{4,5},{5,4},{6,7},{7,6},{8,9},{9,8},{10,11... | collective-permute-start | bytes 3145736 | tf_op jit(solution)/shard_map/ppermute | solution.py:37
  118.6 49.6 %collective-permute-start.54 = (bf16[512,2048]{1,0:T(8,128)(2,1)}, bf16[512,2048]{1,0:T(8,128)(2,1)}, u32[]{:S(2)}, u32[]{:S(2)}) collective-permute-start(bf16[512,2048]{1,0:T(8,128)(2,1)} %bitcast.3.refs_4_), channel_id=1, source_target_pairs={{0,64},{2,66},{4,68},{6,70},{8,72},{10,74},{12,76},{14,78},{16,80}... | collective-permute-start | bytes 6291464 | tf_op jit(solution)/shard_map/ppermute | solution.py:33
  120.4 47.8 %collective-permute-start.31 = (bf16[512,768]{1,0:T(8,128)(2,1)}, bf16[512,768]{1,0:T(8,128)(2,1)}, u32[]{:S(2)}, u32[]{:S(2)}) collective-permute-start(bf16[512,768]{1,0:T(8,128)(2,1)} %get-tuple-element.104), channel_id=1, source_target_pairs={{0,2},{2,4},{4,6},{6,0},{8,10},{10,12},{12,14},{14,8},{16,18},{18,... | collective-permute-start | bytes 2359304 | tf_op jit(solution)/shard_map/ppermute | solution.py:33
  122.3 46.4 %collective-permute-start.32 = (bf16[512,768]{1,0:T(8,128)(2,1)}, bf16[512,768]{1,0:T(8,128)(2,1)}, u32[]{:S(2)}, u32[]{:S(2)}) collective-permute-start(bf16[512,768]{1,0:T(8,128)(2,1)} %get-tuple-element.103), channel_id=1, source_target_pairs={{0,6},{2,0},{4,2},{6,4},{8,14},{10,8},{12,10},{14,12},{16,22},{18,... | collective-permute-start | bytes 2359304 | tf_op jit(solution)/shard_map/ppermute | solution.py:33
  125.0 43.8 %collective-permute-start.33 = (bf16[512,768]{1,0:T(8,128)(2,1)}, bf16[512,768]{1,0:T(8,128)(2,1)}, u32[]{:S(2)}, u32[]{:S(2)}) collective-permute-start(bf16[512,768]{1,0:T(8,128)(2,1)} %get-tuple-element.102), channel_id=1, source_target_pairs={{0,4},{2,6},{4,0},{6,2},{8,12},{10,14},{12,8},{14,10},{16,20},{18,... | collective-permute-start | bytes 2359304 | tf_op jit(solution)/shard_map/ppermute | solution.py:33
  125.5 46.5 %collective-permute-start.43 = (bf16[512,768]{1,0:T(8,128)(2,1)}, bf16[512,768]{1,0:T(8,128)(2,1)}, u32[]{:S(2)}, u32[]{:S(2)}) collective-permute-start(bf16[512,768]{1,0:T(8,128)(2,1)} %get-tuple-element.101), channel_id=1, source_target_pairs={{0,8},{2,10},{4,12},{6,14},{8,16},{10,18},{12,20},{14,22},{16,24},... | collective-permute-start | bytes 2359304 | tf_op jit(solution)/shard_map/ppermute | solution.py:33
  168.2 54.6 %collective-permute-start.2 = (bf16[512,2048]{1,0:T(8,128)(2,1)}, bf16[512,2048]{1,0:T(8,128)(2,1)}, u32[]{:S(2)}, u32[]{:S(2)}) collective-permute-start(bf16[512,2048]{1,0:T(8,128)(2,1)} %add_convert_fusion.1), channel_id=1, source_target_pairs={{0,1},{1,0},{2,3},{3,2},{4,5},{5,4},{6,7},{7,6},{8,9},{9,8},{10,11... | collective-permute-start | bytes 6291464 | tf_op jit(solution)/shard_map/ppermute | solution.py:37
  168.2 52.9 %collective-permute-start.25 = (bf16[256,2048]{1,0:T(8,128)(2,1)}, bf16[256,2048]{1,0:T(8,128)(2,1)S(1)}, u32[]{:S(2)}, u32[]{:S(2)}) collective-permute-start(bf16[256,2048]{1,0:T(8,128)(2,1)} %constant_dynamic-slice_fusion.9), channel_id=1, source_target_pairs={{0,2},{2,4},{4,6},{6,0},{8,10},{10,12},{12,14},{14,8},{16,18},{18,... | collective-permute-start | bytes 3145736 | tf_op jit(solution)/shard_map/ppermute | solution.py:33
  190.3 46.7 %collective-permute-start.26 = (bf16[256,2048]{1,0:T(8,128)(2,1)}, bf16[256,2048]{1,0:T(8,128)(2,1)S(1)}, u32[]{:S(2)}, u32[]{:S(2)}) collective-permute-start(bf16[256,2048]{1,0:T(8,128)(2,1)} %constant_dynamic-slice_fusion.9), channel_id=1, source_target_pairs={{0,6},{2,0},{4,2},{6,4},{8,14},{10,8},{12,10},{14,12},{16,22},{18,... | collective-permute-start | bytes 3145736 | tf_op jit(solution)/shard_map/ppermute | solution.py:33
  222.8 44.4 %collective-permute-start.39 = (bf16[256,2048]{1,0:T(8,128)(2,1)}, bf16[256,2048]{1,0:T(8,128)(2,1)}, u32[]{:S(2)}, u32[]{:S(2)}) collective-permute-start(bf16[256,2048]{1,0:T(8,128)(2,1)} %constant_dynamic-slice_fusion.9), channel_id=1, source_target_pairs={{0,16},{2,18},{4,20},{6,22},{8,24},{10,26},{12,28},{14,30},{16,0},... | collective-permute-start | bytes 3145736 | tf_op jit(solution)/shard_map/ppermute | solution.py:33
  270.7 63.3 %collective-permute-start.40 = (bf16[256,2048]{1,0:T(8,128)(2,1)}, bf16[256,2048]{1,0:T(8,128)(2,1)}, u32[]{:S(2)}, u32[]{:S(2)}) collective-permute-start(bf16[256,2048]{1,0:T(8,128)(2,1)} %collective-permute-done.37.refs_1_), channel_id=1, source_target_pairs={{0,1},{1,0},{2,3},{3,2},{4,5},{5,4},{6,7},{7,6},{8,9},{9,8},{10,11... | collective-permute-start | bytes 3145736 | tf_op jit(solution)/shard_map/ppermute | solution.py:37
  270.7 65.5 %collective-permute-start.41 = (bf16[256,2048]{1,0:T(8,128)(2,1)}, bf16[256,2048]{1,0:T(8,128)(2,1)}, u32[]{:S(2)}, u32[]{:S(2)}) collective-permute-start(bf16[256,2048]{1,0:T(8,128)(2,1)} %collective-permute-done.38.refs_2_), channel_id=1, source_target_pairs={{0,1},{1,0},{2,3},{3,2},{4,5},{5,4},{6,7},{7,6},{8,9},{9,8},{10,11... | collective-permute-start | bytes 3145736 | tf_op jit(solution)/shard_map/ppermute | solution.py:37
  271.2 67.5 %collective-permute-start.42 = (bf16[256,2048]{1,0:T(8,128)(2,1)}, bf16[256,2048]{1,0:T(8,128)(2,1)}, u32[]{:S(2)}, u32[]{:S(2)}) collective-permute-start(bf16[256,2048]{1,0:T(8,128)(2,1)} %collective-permute-done.39.refs_3_), channel_id=1, source_target_pairs={{0,1},{1,0},{2,3},{3,2},{4,5},{5,4},{6,7},{7,6},{8,9},{9,8},{10,11... | collective-permute-start | bytes 3145736 | tf_op jit(solution)/shard_map/ppermute | solution.py:37
  288.4 76.0 %collective-permute-start.57 = (f32[192,2048]{1,0:T(8,128)}, f32[192,2048]{1,0:T(8,128)}, u32[]{:S(2)}, u32[]{:S(2)}) collective-permute-start(f32[192,2048]{1,0:T(8,128)} %get-tuple-element.76), channel_id=1, source_target_pairs={{0,16},{2,18},{4,20},{6,22},{8,24},{10,26},{12,28},{14,30},{16,0},... | collective-permute-start | bytes 4718600 | tf_op jit(solution)/shard_map/ppermute | solution.py:33
  292.8 75.3 %collective-permute-start.56 = (f32[192,2048]{1,0:T(8,128)}, f32[192,2048]{1,0:T(8,128)}, u32[]{:S(2)}, u32[]{:S(2)}) collective-permute-start(f32[192,2048]{1,0:T(8,128)} %get-tuple-element.75), channel_id=1, source_target_pairs={{0,24},{2,26},{4,28},{6,30},{8,0},{10,2},{12,4},{14,6},{16,8},{18,... | collective-permute-start | bytes 4718600 | tf_op jit(solution)/shard_map/ppermute | solution.py:33
  338.7 55.0 %collective-permute-start.36 = (f32[512,768]{1,0:T(8,128)S(1)}, f32[512,768]{1,0:T(8,128)S(1)}, u32[]{:S(2)}, u32[]{:S(2)}) collective-permute-start(f32[512,768]{1,0:T(8,128)S(1)} %copy-done.27), channel_id=1, source_target_pairs={{0,64},{2,66},{4,68},{6,70},{8,72},{10,74},{12,76},{14,78},{16,80}... | collective-permute-start | bytes 4718600 | tf_op jit(solution)/shard_map/ppermute | solution.py:33
  371.3 41.0 %collective-permute-start.35 = (f32[512,768]{1,0:T(8,128)S(1)}, f32[512,768]{1,0:T(8,128)S(1)}, u32[]{:S(2)}, u32[]{:S(2)}) collective-permute-start(f32[512,768]{1,0:T(8,128)S(1)} %copy-done.25), channel_id=1, source_target_pairs={{0,96},{2,98},{4,100},{6,102},{8,104},{10,106},{12,108},{14,110},{... | collective-permute-start | bytes 4718600 | tf_op jit(solution)/shard_map/ppermute | solution.py:33
  380.4 42.1 %collective-permute-start.34 = (f32[512,768]{1,0:T(8,128)S(1)}, f32[512,768]{1,0:T(8,128)}, u32[]{:S(2)}, u32[]{:S(2)}) collective-permute-start(f32[512,768]{1,0:T(8,128)S(1)} %copy-done.23), channel_id=1, source_target_pairs={{0,32},{2,34},{4,36},{6,38},{8,40},{10,42},{12,44},{14,46},{16,48}... | collective-permute-start | bytes 4718600 | tf_op jit(solution)/shard_map/ppermute | solution.py:33
  391.6 70.1 %collective-permute-start.47 = (f32[4,128,768]{2,1,0:T(8,128)S(1)}, f32[4,128,768]{2,1,0:T(8,128)}, u32[]{:S(2)}, u32[]{:S(2)}) collective-permute-start(f32[4,128,768]{2,1,0:T(8,128)S(1)} %get-tuple-element.63), channel_id=1, source_target_pairs={{0,6},{2,0},{4,2},{6,4},{8,14},{10,8},{12,10},{14,12},{16,22},{18,... | collective-permute-start | bytes 4718600 | tf_op jit(solution)/shard_map/ppermute | solution.py:33
  394.9 69.2 %collective-permute-start.46 = (f32[4,128,768]{2,1,0:T(8,128)S(1)}, f32[4,128,768]{2,1,0:T(8,128)}, u32[]{:S(2)}, u32[]{:S(2)}) collective-permute-start(f32[4,128,768]{2,1,0:T(8,128)S(1)} %get-tuple-element.62), channel_id=1, source_target_pairs={{0,2},{2,4},{4,6},{6,0},{8,10},{10,12},{12,14},{14,8},{16,18},{18,... | collective-permute-start | bytes 4718600 | tf_op jit(solution)/shard_map/ppermute | solution.py:33
  413.5 76.7 %collective-permute-start.3 = (bf16[512,2048]{1,0:T(8,128)(2,1)}, bf16[512,2048]{1,0:T(8,128)(2,1)}, u32[]{:S(2)}, u32[]{:S(2)}) collective-permute-start(bf16[512,2048]{1,0:T(8,128)(2,1)} %add_convert_fusion), channel_id=1, source_target_pairs={{0,1},{1,0},{2,3},{3,2},{4,5},{5,4},{6,7},{7,6},{8,9},{9,8},{10,11... | collective-permute-start | bytes 6291464 | tf_op jit(solution)/shard_map/ppermute | solution.py:37
  422.5 105.2 %collective-permute-start.1 = (bf16[512,2048]{1,0:T(8,128)(2,1)}, bf16[512,2048]{1,0:T(8,128)(2,1)S(1)}, u32[]{:S(2)}, u32[]{:S(2)}) collective-permute-start(bf16[512,2048]{1,0:T(8,128)(2,1)} %convolution_convert_fusion.3), channel_id=1, source_target_pairs={{0,1},{1,0},{2,3},{3,2},{4,5},{5,4},{6,7},{7,6},{8,9},{9,8},{10,11... | collective-permute-start | bytes 6291464 | tf_op jit(solution)/shard_map/ppermute | solution.py:37
  429.0 46.2 %collective-permute-start.15 = (f32[4,128,512]{2,1,0:T(8,128)S(1)}, f32[4,128,512]{2,1,0:T(8,128)S(1)}, u32[]{:S(2)}, u32[]{:S(2)}) collective-permute-start(f32[4,128,512]{2,1,0:T(8,128)S(1)} %get-tuple-element.55), channel_id=1, source_target_pairs={{0,16},{2,18},{4,20},{6,22},{8,24},{10,26},{12,28},{14,30},{16,0},... | collective-permute-start | bytes 3145736 | tf_op jit(solution)/shard_map/ppermute | solution.py:33
  475.2 53.6 %collective-permute-start.19 = (bf16[256,2048]{1,0:T(8,128)(2,1)S(1)}, bf16[256,2048]{1,0:T(8,128)(2,1)S(1)}, u32[]{:S(2)}, u32[]{:S(2)}) collective-permute-start(bf16[256,2048]{1,0:T(8,128)(2,1)S(1)} %copy-done.55), channel_id=1, source_target_pairs={{0,32},{2,34},{4,36},{6,38},{8,40},{10,42},{12,44},{14,46},{16,48}... | collective-permute-start | bytes 3145736 | tf_op jit(solution)/shard_map/ppermute | solution.py:33
  485.2 43.6 %collective-permute-start.20 = (bf16[256,2048]{1,0:T(8,128)(2,1)S(1)}, bf16[256,2048]{1,0:T(8,128)(2,1)S(1)}, u32[]{:S(2)}, u32[]{:S(2)}) collective-permute-start(bf16[256,2048]{1,0:T(8,128)(2,1)S(1)} %copy-done.55), channel_id=1, source_target_pairs={{0,96},{2,98},{4,100},{6,102},{8,104},{10,106},{12,108},{14,110},{... | collective-permute-start | bytes 3145736 | tf_op jit(solution)/shard_map/ppermute | solution.py:33
  488.3 41.1 %collective-permute-start.21 = (bf16[256,2048]{1,0:T(8,128)(2,1)S(1)}, bf16[256,2048]{1,0:T(8,128)(2,1)S(1)}, u32[]{:S(2)}, u32[]{:S(2)}) collective-permute-start(bf16[256,2048]{1,0:T(8,128)(2,1)S(1)} %copy-done.55), channel_id=1, source_target_pairs={{0,64},{2,66},{4,68},{6,70},{8,72},{10,74},{12,76},{14,78},{16,80}... | collective-permute-start | bytes 3145736 | tf_op jit(solution)/shard_map/ppermute | solution.py:33
  (101 other events, 1874.4 us)
